TPU v7x, 32 devices: a whole 2x2x4 slice. The times are simulated.
32 devices in a mesh: dp: 16 (over z, x, core), tensor: 2 (over y).
Axes of the slice: x: 2, y: 2, z: 4, core: 2. Of those that a mesh axis runs over, the one named last changes fastest.
Arguments:
- inputs: bfloat16 [4096, 1792], P(('dp', 'tensor')), may hold values from -6 to 6
- cotangent: bfloat16 [4096, 1792], P(('dp', 'tensor')), may hold values from -6 to 6
- segments: int32 [16, 256], P('dp'), may hold values from 0 to 2, never falling along the last dimension, each value on 1 to 128 neighbouring positions
- slot_conv: int32 [294], replicated, may hold values from 0 to 367, as said below
- slot_mix: int32 [420], replicated, may hold values from 0 to 527, as said below
- slot_mlp: int32 [798], replicated, may hold values from 0 to 1007, as said below
- state_conv: float32 [3, 368, 32768], P(None, 'dp', 'tensor')
- state_mix: float32 [3, 528, 32768], P(None, 'dp', 'tensor'), as said below
- state_mlp: float32 [3, 1008, 32768], P(None, 'dp', 'tensor')
- small_state: float32 [3, 6, 1792], replicated, as said below
Outputs:
- result: bfloat16 [4096, 1792], P(('dp', 'tensor'))
- grad_input: float32 [4096, 1792], P(('dp', 'tensor'))
- new_conv: float32 [3, 368, 32768], P(None, 'dp', 'tensor')
- new_mix: float32 [3, 528, 32768], P(None, 'dp', 'tensor')
- new_mlp: float32 [3, 1008, 32768], P(None, 'dp', 'tensor')
- new_small: float32 [2, 6, 1792], replicated
- small_update: float32 [6, 1792], replicated
Inputs may be any that keep to these rules, and one draw needn't show every extreme that they name: `slot_conv`: distinct slot numbers; the owner of a unit is the dp index slot // 23, so that every owner holds at most 23 units and one owner holds exactly 23. The first and the last slot are always used. `slot_mix`: distinct slot numbers; the owner of a unit is slot // 33, at most 33 units an owner, one owner holding exactly 33. The first and the last slot are always used. `slot_mlp`: distinct slot numbers; the owner of a unit is slot // 63, at most 63 units an owner, one owner holding exactly 63. The first and the last slot are always used. `state_mix`: the second moments (index 2) are positive. `small_state`: the second moments (index 2) are positive.
All inputs are finite; a program needn't handle non-finite values.
Results may differ from a plain program's by a relative error of at most 0.025.
Values may be sent and summed in bfloat16 or wider, within the bound.
A program may use at most 384 MiB of HBM per device.

v0:
```python
import math

import functools

import jax
import jax.numpy as jnp
from jax import lax
from jax.experimental import pallas as pl
from jax.experimental.pallas import tpu as pltpu
from jax.sharding import PartitionSpec as P

MESH = pl.DeviceIdType.MESH
LANES = 128

D = 1792
HEADS = 16
FEAT = 16
FF = 4864
WINDOW = 64
TAPS = 3
STEP = 5
HEAD = 112


NORM_EPS = 1e-05
BETA_ONE = 0.9
BETA_TWO = 0.95
ADAM_EPS = 1e-08
LEARN_RATE = 0.02
SMALL_RATE = 0.16
WEIGHT_DECAY = 0.1
NEG_FILL = -1e30
CONV_SCALE = 0.125
MIX_SCALE = 0.25
MLP_SCALE = 0.5
SMALL_SCALE = 0.125


def norm_rows(values, gain):
    return values * lax.rsqrt(jnp.mean(values * values, axis=-1, keepdims=True) + NORM_EPS) * gain


def norm_back(values, gain, upstream):
    _, pullback = jax.vjp(norm_rows, values, gain)
    return pullback(upstream)


def product(left, right):
    return jnp.dot(left, right, preferred_element_type=jnp.float32)


def product_left(left, right):
    return lax.dot_general(
        left, right, (((0,), (0,)), ((), ())), preferred_element_type=jnp.float32
    )


def product_right(left, right):
    return lax.dot_general(
        left, right, (((1,), (1,)), ((), ())), preferred_element_type=jnp.float32
    )


def swap(values, axis, bit):
    size = lax.axis_size(axis)
    return lax.ppermute(values, axis, [(i, i ^ bit) for i in range(size)])


def gather_rows(piece_rows):
    other = swap(piece_rows, "tensor", 1)
    first = lax.axis_index("tensor") == 0
    return jnp.concatenate(
        [jnp.where(first, piece_rows, other), jnp.where(first, other, piece_rows)]
    )


def sum_rows(piece_rows):
    rows = piece_rows.shape[0] // 2
    at = lax.axis_index("tensor")
    halves = piece_rows.astype(jnp.bfloat16).reshape(2, rows, piece_rows.shape[1])
    other = swap(lax.dynamic_index_in_dim(halves, 1 - at, 0, False), "tensor", 1)
    mine = lax.dynamic_index_in_dim(halves, at, 0, False)
    return mine.astype(jnp.float32) + other.astype(jnp.float32)


def delayed(values, steps):
    return jnp.pad(values, ((steps, 0), (0, 0)))[: values.shape[0]]


def advanced(values, steps):
    return jnp.pad(values, ((0, steps), (0, 0)))[steps:]


def lay_body(parts, slots_ref, pooled_ref, *refs):
    out_refs, (buf, stage, sem) = refs[: len(parts)], refs[len(parts) :]
    step = pl.program_id(0)
    depth = buf.shape[2]
    starts = [sum(part[4] for part in parts[:p]) for p in range(len(parts))]

    def inside(at, p):
        return (at >= starts[p]) & (at < starts[p] + parts[p][4])

    def fetch(at, half):
        for p, (first, nu, blocks, _, _) in enumerate(parts):

            @pl.when(inside(at, p))
            def _():
                for q in range(nu * blocks):
                    unit = first + (at - starts[p]) * (nu * blocks) + q
                    pltpu.make_async_copy(
                        pooled_ref.at[slots_ref[unit]], buf.at[half, q], sem.at[half]
                    ).start()

    @pl.when(step == 0)
    def _():
        fetch(0, 0)

    @pl.when(step + 1 < pl.num_programs(0))
    def _():
        fetch(step + 1, (step + 1) % 2)

    half = step % 2
    for p, (first, nu, blocks, m, _) in enumerate(parts):
        out_ref = out_refs[p]
        rows = nu * depth // m

        @pl.when(inside(step, p))
        def _():
            pltpu.make_async_copy(
                pooled_ref.at[pl.ds(0, nu * blocks)], buf.at[half, pl.ds(0, nu * blocks)], sem.at[half]
            ).wait()
            for block in range(blocks):
                if m == 1:
                    for q in range(nu):
                        at = (block * nu + q) * depth
                        out_ref[at : at + depth, :] = buf[half, block * nu + q]
                    continue
                base = (block % 2) * stage.shape[0] // 2
                for q in range(nu):
                    at = base + q * depth
                    stage[at : at + depth, :] = buf[half, block * nu + q].astype(jnp.float32)
                for c in range(m):
                    out_ref[block * rows : (block + 1) * rows, c * LANES : (c + 1) * LANES] = stage[
                        pl.ds(base + c, rows, stride=m), :
                    ].astype(jnp.bfloat16)


def lay_out(pooled, slots, wanted):
    depth = pooled.shape[1]
    parts, specs, shapes = [], [], []
    first = start = 0
    for count, width, nu, blocks in wanted:
        m = width // LANES
        steps = count // (nu * blocks)
        rows = nu * blocks * depth // m
        assert steps * nu * blocks == count
        parts.append((first, nu, blocks, m, steps))

        def place(i, s, start=start, steps=steps):
            return (jnp.clip(i - start, 0, steps - 1), 0)

        specs.append(pl.BlockSpec((rows, width), place))
        shapes.append(jax.ShapeDtypeStruct((steps * rows, width), jnp.bfloat16))
        first += count
        start += steps
    return pl.pallas_call(
        functools.partial(lay_body, tuple(parts)),
        grid_spec=pltpu.PrefetchScalarGridSpec(
            num_scalar_prefetch=1,
            grid=(start,),
            in_specs=[pl.BlockSpec(memory_space=pl.ANY)],
            out_specs=specs,
            scratch_shapes=[
                pltpu.VMEM((2, max(p[1] * p[2] for p in parts), depth, LANES), jnp.bfloat16),
                pltpu.VMEM((2 * max(p[1] for p in parts) * depth, LANES), jnp.float32),
                pltpu.SemaphoreType.DMA((2,)),
            ],
        ),
        out_shape=shapes,
        cost_estimate=pl.CostEstimate(
            flops=0, bytes_accessed=4 * first * depth * LANES, transcendentals=0
        ),
        name=f"lay_{first}",
    )(slots, pooled)


def grad_body(parts, sources, slots_ref, *refs):
    ins, out_ref, stage = refs[:sources], refs[sources], refs[sources + 1]
    bufs, sem = refs[sources + 2 : -1], refs[-1]
    depth = LANES

    def drain(p, half):
        nu = bufs[p].shape[1]
        pltpu.make_async_copy(out_ref.at[pl.ds(0, nu)], bufs[p].at[half], sem.at[p, half]).wait()

    for p, (first, rows, left, right) in enumerate(parts):
        u_ref, d_ref, buf = ins[left], ins[right], bufs[p]
        m = d_ref.shape[1] // LANES
        nu = rows * m // depth

        def step_of(step, carry):
            half = step % 2

            @pl.when(step >= 2)
            def _():
                drain(p, half)

            at = pl.multiple_of(step * rows, LANES)
            turned = u_ref[:, pl.ds(at, rows)].T
            for c in range(0, m, 2):
                wide = min(2, m - c)
                piece = jnp.dot(
                    turned,
                    d_ref[:, c * LANES : (c + wide) * LANES],
                    preferred_element_type=jnp.float32,
                )
                for k in range(wide):
                    part = piece[:, k * LANES : (k + 1) * LANES]
                    if m == 1:
                        stage[:rows, :] = part
                    else:
                        stage[pl.ds(c + k, rows, stride=m), :] = part
            for q in range(nu):
                buf[half, q] = stage[q * depth : (q + 1) * depth, :].astype(jnp.bfloat16)
            for q in range(nu):
                pltpu.make_async_copy(
                    buf.at[half, q], out_ref.at[slots_ref[first + step * nu + q]], sem.at[p, half]
                ).start()
            return carry

        lax.fori_loop(0, u_ref.shape[1] // rows, step_of, 0)
    for p, (first, rows, left, right) in enumerate(parts):
        steps = ins[left].shape[1] // rows
        drain(p, (steps - 1) % 2)
        if steps > 1:
            drain(p, steps % 2)


def grad_units(slot_rows, slots, wanted):
    operands, parts, bufs = [], [], []
    first = most = flops = 0
    where = {}
    for u, d, rows in wanted:
        for value in (u, d):
            if id(value) not in where:
                where[id(value)] = len(operands)
                operands.append(value)
        height, width = u.shape[1], d.shape[1]
        nu = rows * width // LANES // LANES
        parts.append((first, rows, where[id(u)], where[id(d)]))
        bufs.append(pltpu.VMEM((2, nu, LANES, LANES), jnp.bfloat16))
        first += height * width // LANES // LANES
        most = max(most, nu)
        flops += 2 * u.shape[0] * height * width
    return pl.pallas_call(
        functools.partial(grad_body, tuple(parts), len(operands)),
        grid_spec=pltpu.PrefetchScalarGridSpec(
            num_scalar_prefetch=1,
            in_specs=[pl.BlockSpec(memory_space=pltpu.VMEM)] * len(operands),
            out_specs=pl.BlockSpec(memory_space=pl.ANY),
            scratch_shapes=[
                pltpu.VMEM((most * LANES, LANES), jnp.float32),
                *bufs,
                pltpu.SemaphoreType.DMA((len(parts), 2)),
            ],
        ),
        out_shape=jax.ShapeDtypeStruct((slot_rows, LANES, LANES), jnp.bfloat16),
        cost_estimate=pl.CostEstimate(
            flops=flops, bytes_accessed=2 * first * LANES * LANES, transcendentals=0
        ),
        name=f"grad_{first}",
    )(slots, *operands)


def bits_of(owners):
    return owners.bit_length() - 1


def chunks_of(total, most):
    number = -(-total // most)
    base, extra = divmod(total, number)
    out, at = [], 0
    for k in range(number):
        size = base + (1 if k < extra else 0)
        out.append((at, size))
        at += size
    return out


def scatter_body(owners, caps, jobs, *refs):
    stages = bits_of(owners)
    groups = len(caps)
    g_refs, small_ref = refs[:groups], refs[groups]
    out_refs, small_out = refs[groups + 1 : 2 * groups + 1], refs[2 * groups + 1]
    refs = refs[2 * groups + 2 :]
    landing = [refs[s * groups : (s + 1) * groups] for s in range(stages)]
    own, small_sum, small_land, send_sem, recv_sem, own_sem, small_send, small_recv = refs[
        stages * groups :
    ]
    me = lax.axis_index("dp")
    ten = lax.axis_index("tensor")
    bit = [(me // (1 << s)) % 2 for s in range(stages)]
    partner = [me + (1 - 2 * bit[s]) * (1 << s) for s in range(stages)]
    barrier = pltpu.get_barrier_semaphore()
    for s in range(stages):
        pl.semaphore_signal(barrier, inc=1, device_id=(partner[s], ten), device_id_type=MESH)
    pl.semaphore_signal(barrier, inc=1, device_id=(me, 1 - ten), device_id_type=MESH)
    pl.semaphore_wait(barrier, stages + 1)
    count = len(jobs)

    def small(s):
        to = (me, 1 - ten) if s == stages else (partner[s], ten)
        return pltpu.make_async_remote_copy(
            src_ref=small_ref if s == 0 else small_sum.at[s - 1],
            dst_ref=small_land.at[s],
            send_sem=small_send.at[s],
            recv_sem=small_recv.at[s],
            device_id=to,
            device_id_type=MESH,
        )

    def small_step(s):
        small(s).wait_recv()
        total = (small_ref[...] if s == 0 else small_sum[s - 1]) + small_land[s]
        if s == stages:
            small_out[...] = total
        else:
            small_sum[s] = total
            small(s + 1).start()

    small(0).start()

    def bit_at(s, k):
        if jobs[k][3] and s in (1, 2):
            return 3 - s
        return s

    def sides(s, k):
        before = owners >> s
        inner = 2 if jobs[k][3] and s == 1 else 1
        return before // 2 // inner, inner

    def part(s, k, which):
        g, at, size, _ = jobs[k]
        outer, inner = sides(s, k)
        span = pl.ds(at, size)
        if s == 0:
            return g_refs[g].at[:, which, span]
        ref = landing[s - 1][g]
        view = ref.reshape(outer, 2, inner, *ref.shape[1:])
        return view.at[:, which, :, span]

    def remote(s, k):
        g, at, size, _ = jobs[k]
        outer, inner = sides(s, k)
        span = pl.ds(at, size)
        b = bit_at(s, k)
        ref = landing[s][g]
        dst = ref.at[:, span] if s == 0 else ref.reshape(outer, inner, *ref.shape[1:]).at[:, :, span]
        return pltpu.make_async_remote_copy(
            src_ref=part(s, k, 1 - bit[b]),
            dst_ref=dst,
            send_sem=send_sem.at[s, k],
            recv_sem=recv_sem.at[s, k],
            device_id=(partner[b], ten),
            device_id_type=MESH,
        )

    def local(k):
        return pltpu.make_async_copy(
            part(0, k, bit[0]), own.at[k % 2, :, pl.ds(0, jobs[k][2])], own_sem.at[k % 2]
        )

    for k in range(count):
        remote(0, k).start()
    local(0).start()

    def work(s, k):
        g, at, size, _ = jobs[k]
        left = owners >> (s + 1)
        outer, inner = sides(s, k)
        if s == 0:
            if k + 1 < count:
                local(k + 1).start()
            local(k).wait()
        remote(s, k).wait_recv()
        mine_bit = bit[bit_at(s, k)]
        into = landing[s][g]

        def add(j, carry):
            o, u = j // size, j % size
            if s == 0:
                mine = own[k % 2, o, u]
            else:
                mine = landing[s - 1][g][(o // inner) * 2 * inner + mine_bit * inner + o % inner, at + u]
            total = into[o, at + u].astype(jnp.float32) + mine.astype(jnp.float32)
            if s == stages - 1:
                out_refs[g][at + u] = total
            else:
                into[o, at + u] = total.astype(jnp.bfloat16)
            return carry

        lax.fori_loop(0, left * size, add, 0)
        if s + 1 < stages:
            remote(s + 1, k).start()

    lag = 2
    for t in range(count + lag * (stages - 1)):
        for s in range(stages):
            k = t - lag * s
            if 0 <= k < count:
                work(s, k)
        if t % 2 == 1 and t // 2 <= stages:
            small_step(t // 2)
    for s in range(stages):
        for k in range(count):
            remote(s, k).wait_send()
    for s in range(stages + 1):
        small(s).wait_send()


def scatter_sum(units, small, owners, caps, collective=1, most=4):
    stages = bits_of(owners)
    depth, lanes = units[0].shape[1:]
    jobs = []
    for g, cap in enumerate(caps):
        for at, size in chunks_of(cap, most):
            jobs.append((g, at, size, stages > 2 and len(jobs) % 4 == 2))
    widest = max(size for _, _, size, _ in jobs)
    assert len(jobs) + 2 * (stages - 1) > 2 * stages + 1
    scratch = []
    for s in range(stages):
        for cap in caps:
            scratch.append(pltpu.VMEM((owners >> (s + 1), cap, depth, lanes), jnp.bfloat16))
    scratch += [
        pltpu.VMEM((2, owners // 2, widest, depth, lanes), jnp.bfloat16),
        pltpu.VMEM((stages, *small.shape), jnp.float32),
        pltpu.VMEM((stages + 1, *small.shape), jnp.float32),
        pltpu.SemaphoreType.DMA((stages, len(jobs))),
        pltpu.SemaphoreType.DMA((stages, len(jobs))),
        pltpu.SemaphoreType.DMA((2,)),
        pltpu.SemaphoreType.DMA((stages + 1,)),
        pltpu.SemaphoreType.DMA((stages + 1,)),
    ]
    return pl.pallas_call(
        functools.partial(scatter_body, owners, caps, tuple(jobs)),
        out_shape=[
            *[jax.ShapeDtypeStruct((cap, depth, lanes), jnp.float32) for cap in caps],
            jax.ShapeDtypeStruct(small.shape, jnp.float32),
        ],
        in_specs=[
            *[pl.BlockSpec(memory_space=pl.ANY)] * len(caps),
            pl.BlockSpec(memory_space=pltpu.VMEM),
        ],
        out_specs=[pl.BlockSpec(memory_space=pltpu.VMEM)] * (len(caps) + 1),
        scratch_shapes=scratch,
        compiler_params=pltpu.CompilerParams(collective_id=collective, has_side_effects=True),
        name="scatter_sum",
    )(
        *[group.reshape(owners // 2, 2, cap, depth, lanes) for group, cap in zip(units, caps)],
        small,
    )


def adam_values(master, one, two, gradient, rate):
    moment_one = BETA_ONE * one + (1.0 - BETA_ONE) * gradient
    moment_two = BETA_TWO * two + (1.0 - BETA_TWO) * gradient * gradient
    step_size = (
        moment_one
        / (1.0 - BETA_ONE**STEP)
        / (jnp.sqrt(moment_two / (1.0 - BETA_TWO**STEP)) + ADAM_EPS)
    )
    return master - rate * (step_size + WEIGHT_DECAY * master), moment_one, moment_two


def adam_step(opt_state, gradient, rate):
    return jnp.stack(adam_values(opt_state[0], opt_state[1], opt_state[2], gradient, rate))


def adam_body(scale, used_ref, state_ref, summed_ref, out_ref):
    cap, rows, lanes = summed_ref.shape
    flat = summed_ref.reshape(cap * rows, lanes)
    used = used_ref[...] > 0
    for r in range(rows):
        here = slice(r * lanes, (r + 1) * lanes)
        summed = flat[pl.ds(r, cap, stride=rows), :] * scale
        gradient = jnp.where(used, summed, 0.0)
        new = adam_values(
            state_ref[0, :, here], state_ref[1, :, here], state_ref[2, :, here], gradient, LEARN_RATE
        )
        for k in range(3):
            out_ref[k, :, here] = new[k]


def adam_units(state, summed, slots, scale):
    cap, unit_width = state.shape[1:]
    mine = lax.axis_index("dp") * cap + jnp.arange(cap, dtype=jnp.int32)
    used = jnp.any(mine[:, None] == slots[None, :], axis=1).astype(jnp.int32)
    rows = 16
    block = rows * LANES
    return pl.pallas_call(
        functools.partial(adam_body, scale),
        grid=(unit_width // block,),
        in_specs=[
            pl.BlockSpec((cap, LANES), lambda i: (0, 0)),
            pl.BlockSpec((3, cap, block), lambda i: (0, 0, i)),
            pl.BlockSpec((cap, rows, LANES), lambda i: (0, i, 0)),
        ],
        out_specs=pl.BlockSpec((3, cap, block), lambda i: (0, 0, i)),
        out_shape=jax.ShapeDtypeStruct(state.shape, jnp.float32),
        name=f"adam_{cap}",
    )(jnp.broadcast_to(used[:, None], (cap, LANES)), state, summed)


def gather_units(state, scale):
    cap, unit_width = state.shape[1:]
    own = (state[0] * scale).reshape(cap, unit_width // LANES, LANES).astype(jnp.bfloat16)
    return lax.all_gather(own, "dp", axis=0, tiled=True)


def attend(query_f, key_f, query_s, key_s, lin_mask, win_mask):
    lin_score = jnp.einsum(
        "shf,thf->hst", query_f, key_f, preferred_element_type=jnp.float32
    ) / math.sqrt(FEAT)
    kernel = (1.0 + lin_score + 0.5 * lin_score * lin_score) * lin_mask
    lin_denom = jnp.sum(kernel, axis=-1, keepdims=True)
    lin_prob = kernel / lin_denom
    win_score = jnp.einsum(
        "shd,thd->hst", query_s, key_s, preferred_element_type=jnp.float32
    ) / math.sqrt(HEAD)
    inside = win_mask > 0
    win_peak = jnp.max(jnp.where(inside, win_score, NEG_FILL), axis=-1, keepdims=True)
    win_exp = jnp.exp(jnp.where(inside, win_score - win_peak, NEG_FILL))
    win_prob = win_exp / jnp.sum(win_exp, axis=-1, keepdims=True)
    return (lin_score, lin_denom, lin_prob, win_prob)


def per_device(
    inputs,
    cotangent,
    segments,
    slot_conv,
    slot_mix,
    slot_mlp,
    state_conv,
    state_mix,
    state_mlp,
    small_state,
):
    tensor_size = lax.axis_size("tensor")
    owners = lax.axis_size("dp")
    half_width = D // tensor_size
    local_heads = HEADS // tensor_size
    feat_cols = local_heads * FEAT
    ff_half = FF // tensor_size
    unit_width = state_conv.shape[2]
    cap_conv = state_conv.shape[1]
    cap_mix = state_mix.shape[1]
    cap_mlp = state_mlp.shape[1]
    pooled = (
        gather_units(state_conv, CONV_SCALE),
        gather_units(state_mix, MIX_SCALE),
        gather_units(state_mlp, MLP_SCALE),
    )
    per = D * LANES // unit_width
    narrow, middle = per * feat_cols // LANES, per * half_width // LANES
    wide = per * ff_half // LANES
    conv_pair, conv_back = lay_out(
        pooled[0], slot_conv, ((2 * middle, half_width, 7, 2), (middle, D, 7, 2))
    )
    conv_w = [conv_pair[:D], conv_pair[D:], conv_back]
    feat_pair, mix_trio, mix_back = lay_out(
        pooled[1],
        slot_mix,
        ((2 * narrow, feat_cols, 7, 2), (3 * middle, half_width, 7, 3), (middle, D, 7, 2)),
    )
    mix_w = [
        feat_pair[:D],
        feat_pair[D:],
        mix_trio[:D],
        mix_trio[D : 2 * D],
        mix_trio[2 * D :],
        mix_back,
    ]
    mlp_pair, mlp_back = lay_out(
        pooled[2], slot_mlp, ((2 * wide, ff_half, 19, 2), (wide, D, 7, 2))
    )
    mlp_w = [mlp_pair[:D], mlp_pair[D:], mlp_back]
    params = small_state[0] * SMALL_SCALE
    seg_ids = segments[0]
    length = seg_ids.shape[0]
    positions = jnp.arange(length)
    causal = (positions[:, None] >= positions[None, :]) & (seg_ids[:, None] == seg_ids[None, :])
    lin_mask = causal.astype(jnp.float32)
    win_mask = (causal & (positions[:, None] - positions[None, :] < WINDOW)).astype(jnp.float32)
    same_prev = [None]
    for shift_by in range(1, TAPS):
        earlier = jnp.pad(seg_ids, (shift_by, 0), constant_values=-1)[:length]
        same_prev.append((earlier == seg_ids).astype(jnp.float32)[:, None])
    column = lax.axis_index("tensor") * half_width
    taps_local = lax.dynamic_slice_in_dim(params[3:], column, half_width, 1)
    x_rows = inputs.astype(jnp.float32)
    normed_one = norm_rows(x_rows, params[0]).astype(jnp.bfloat16)
    conv_in = gather_rows(normed_one)
    value_c = product(conv_in, conv_w[0])
    gate_c = product(conv_in, conv_w[1])
    mixed_c = taps_local[0] * value_c
    for shift_by in range(1, TAPS):
        mixed_c = mixed_c + taps_local[shift_by] * delayed(value_c, shift_by) * same_prev[shift_by]
    gated_conv = (mixed_c * gate_c).astype(jnp.bfloat16)
    hidden_one = x_rows + sum_rows(product(gated_conv, conv_w[2]))
    normed_two = norm_rows(hidden_one, params[1]).astype(jnp.bfloat16)
    mix_in = gather_rows(normed_two)
    projected = [product(mix_in, weight).astype(jnp.bfloat16) for weight in mix_w[:5]]
    query_f = projected[0].reshape(length, local_heads, FEAT)
    key_f = projected[1].reshape(length, local_heads, FEAT)
    query_s = projected[2].reshape(length, local_heads, HEAD)
    key_s = projected[3].reshape(length, local_heads, HEAD)
    values_v = projected[4].reshape(length, local_heads, HEAD)
    _, _, lin_prob, win_prob = attend(query_f, key_f, query_s, key_s, lin_mask, win_mask)
    attended = jnp.einsum(
        "hst,thd->shd", lin_prob.astype(jnp.bfloat16), values_v, preferred_element_type=jnp.float32
    ) + jnp.einsum(
        "hst,thd->shd", win_prob.astype(jnp.bfloat16), values_v, preferred_element_type=jnp.float32
    )
    mix_out = attended.reshape(length, half_width).astype(jnp.bfloat16)
    hidden_two = hidden_one + sum_rows(product(mix_out, mix_w[5]))
    normed_three = norm_rows(hidden_two, params[2]).astype(jnp.bfloat16)
    ff_in = gather_rows(normed_three)
    gate_proj = product(ff_in, mlp_w[0])
    up_proj = product(ff_in, mlp_w[1])
    activated = (jax.nn.silu(gate_proj) * up_proj).astype(jnp.bfloat16)
    result = (hidden_two + sum_rows(product(activated, mlp_w[2]))).astype(jnp.bfloat16)
    back_three = gather_rows(cotangent)
    back_act = product_right(back_three, mlp_w[2])
    gate_sig = jax.nn.sigmoid(gate_proj)
    back_gate = (back_act * up_proj * gate_sig * (1.0 + gate_proj * (1.0 - gate_sig))).astype(
        jnp.bfloat16
    )
    back_up = (back_act * gate_proj * gate_sig).astype(jnp.bfloat16)
    back_normed_three = sum_rows(
        product_right(back_gate, mlp_w[0]) + product_right(back_up, mlp_w[1])
    )
    back_norm_three, gain_three = norm_back(hidden_two, params[2], back_normed_three)
    back_hidden_two = cotangent.astype(jnp.float32) + back_norm_three
    mlp_units = grad_units(
        owners * cap_mlp,
        slot_mlp,
        (
            (ff_in, back_gate, 2 * LANES),
            (ff_in, back_up, 2 * LANES),
            (activated, back_three, LANES),
        ),
    )
    summed_mlp = lax.psum_scatter(
        mlp_units, "dp", scatter_dimension=0, tiled=True
    ).astype(jnp.float32)
    back_two = gather_rows(back_hidden_two.astype(jnp.bfloat16))
    back_attended = (
        product_right(back_two, mix_w[5]).astype(jnp.bfloat16).reshape(length, local_heads, HEAD)
    )
    lin_again, denom_again, lin_back, win_back = attend(
        query_f, key_f, query_s, key_s, lin_mask, win_mask
    )
    back_prob = jnp.einsum(
        "shd,thd->hst", back_attended, values_v, preferred_element_type=jnp.float32
    )
    back_values = jnp.einsum(
        "hst,shd->thd",
        lin_back.astype(jnp.bfloat16),
        back_attended,
        preferred_element_type=jnp.float32,
    ) + jnp.einsum(
        "hst,shd->thd",
        win_back.astype(jnp.bfloat16),
        back_attended,
        preferred_element_type=jnp.float32,
    )
    back_kernel = (back_prob - jnp.sum(back_prob * lin_back, axis=-1, keepdims=True)) / denom_again
    back_score = (back_kernel * (1.0 + lin_again) * lin_mask).astype(jnp.bfloat16)
    back_query_f = jnp.einsum(
        "hst,thf->shf", back_score, key_f, preferred_element_type=jnp.float32
    ) / math.sqrt(FEAT)
    back_key_f = jnp.einsum(
        "hst,shf->thf", back_score, query_f, preferred_element_type=jnp.float32
    ) / math.sqrt(FEAT)
    back_local = (
        win_back * (back_prob - jnp.sum(back_prob * win_back, axis=-1, keepdims=True))
    ).astype(jnp.bfloat16)
    back_query_s = jnp.einsum(
        "hst,thd->shd", back_local, key_s, preferred_element_type=jnp.float32
    ) / math.sqrt(HEAD)
    back_key_s = jnp.einsum(
        "hst,shd->thd", back_local, query_s, preferred_element_type=jnp.float32
    ) / math.sqrt(HEAD)
    back_projected = [
        piece_grad.reshape(length, -1).astype(jnp.bfloat16)
        for piece_grad in (back_query_f, back_key_f, back_query_s, back_key_s, back_values)
    ]
    back_normed_two = product_right(back_projected[0], mix_w[0])
    for piece_grad, weight in zip(back_projected[1:], mix_w[1:5]):
        back_normed_two = back_normed_two + product_right(piece_grad, weight)
    back_normed_two = sum_rows(back_normed_two)
    back_norm_two, gain_two = norm_back(hidden_one, params[1], back_normed_two)
    back_hidden_one = back_hidden_two + back_norm_two
    mix_units = grad_units(
        owners * cap_mix,
        slot_mix,
        (
            (mix_in, back_projected[0], 7 * LANES),
            (mix_in, back_projected[1], 7 * LANES),
            *[(mix_in, piece_grad, 2 * LANES) for piece_grad in back_projected[2:]],
            (mix_out, back_two, LANES),
        ),
    )
    back_one = gather_rows(back_hidden_one.astype(jnp.bfloat16))
    back_gated = product_right(back_one, conv_w[2])
    back_mixed = back_gated * gate_c
    back_gate_c = (back_gated * mixed_c).astype(jnp.bfloat16)
    back_value_f = taps_local[0] * back_mixed
    tap_grads = [jnp.sum(back_mixed * value_c, axis=0)]
    for shift_by in range(1, TAPS):
        masked = back_mixed * same_prev[shift_by]
        back_value_f = back_value_f + taps_local[shift_by] * advanced(masked, shift_by)
        tap_grads.append(jnp.sum(masked * delayed(value_c, shift_by), axis=0))
    back_value_c = back_value_f.astype(jnp.bfloat16)
    back_normed_one = sum_rows(
        product_right(back_value_c, conv_w[0]) + product_right(back_gate_c, conv_w[1])
    )
    back_norm_one, gain_one = norm_back(x_rows, params[0], back_normed_one)
    grad_input = back_hidden_one + back_norm_one
    conv_units = grad_units(
        owners * cap_conv,
        slot_conv,
        (
            (conv_in, back_value_c, 2 * LANES),
            (conv_in, back_gate_c, 2 * LANES),
            (gated_conv, back_one, LANES),
        ),
    )
    taps_full = lax.dynamic_update_slice(
        jnp.zeros((TAPS, D), jnp.float32), jnp.stack(tap_grads), (jnp.int32(0), column)
    )
    small_grad = jnp.concatenate([jnp.stack([gain_one, gain_two, gain_three]), taps_full], axis=0)
    summed_mix, summed_conv, small_summed = scatter_sum(
        (mix_units, conv_units), small_grad, owners, (cap_mix, cap_conv)
    )
    new_conv = adam_units(state_conv, summed_conv, slot_conv, CONV_SCALE / owners)
    new_mix = adam_units(state_mix, summed_mix, slot_mix, MIX_SCALE / owners)
    new_mlp = adam_units(state_mlp, summed_mlp, slot_mlp, MLP_SCALE / owners)
    small_new = adam_step(small_state, small_summed * (SMALL_SCALE / owners), SMALL_RATE)
    return (
        result,
        grad_input,
        new_conv,
        new_mix,
        new_mlp,
        small_new[1:],
        small_new[0] - small_state[0],
    )


def solution(mesh):
    placed = (
        P(("dp", "tensor"), None),
        P(("dp", "tensor"), None),
        P("dp", None),
        P(),
        P(),
        P(),
        P(None, "dp", "tensor"),
        P(None, "dp", "tensor"),
        P(None, "dp", "tensor"),
        P(),
    )
    return jax.shard_map(
        per_device,
        mesh=mesh,
        in_specs=placed,
        out_specs=(
            P(("dp", "tensor"), None),
            P(("dp", "tensor"), None),
            P(None, "dp", "tensor"),
            P(None, "dp", "tensor"),
            P(None, "dp", "tensor"),
            P(),
            P(),
        ),
        check_vma=False,
    )
```

profile of v0, /device:TPU:15, one launch (start us, length us, event | category | flops | bytes accessed | tf_op | source)
XLA Modules:
  0.0 922.6 jit_solution(16143393324477125562)
XLA Ops:
  13.3 2.4 multiply_convert_fusion
  19.8 11.0 %collective-permute-done = bf16[128,1792]{1,0:T(8,128)(2,1)S(1)} collective-permute-done((bf16[128,1792]{1,0:T(8,128)(2,1)S(1)}, bf16[128,1792]{1,0:T(8,128)(2,1)S(1)}, u32[]{:S(2)}, u32[]{:S(2)}) %collective-permute-start) | collective-permute-done | bytes 458784 | tf_op jit(solution)/shard_map/ppermute | solution.py:66
  31.1 76.5 %all-gather.4.cloned.1.call-done.pooled_ref = bf16[368,128,128]{2,1,0:T(8,128)(2,1)} async-done(((bf16[23,128,128]{2,1,0:T(8,128)(2,1)}), bf16[368,128,128]{2,1,0:T(8,128)(2,1)}) %all-gather.4.cloned.1.call-update) | async-done | bytes 12058640 | tf_op jit(solution)/shard_map/all_gather | solution.py:518
  107.7 16.1 %lay_294.1 = (bf16[3584,896]{1,0:T(8,128)(2,1)}, bf16[896,1792]{1,0:T(8,128)(2,1)}) custom-call(s32[294]{0:T(512)} %slots_ref.10, bf16[368,128,128]{2,1,0:T(8,128)(2,1)} %all-gather.4.cloned.1.call-done.pooled_ref), custom_call_target="tpu_custom_call" | custom-call | bytes 19267584 | tf_op jit(solution)/shard_map/lay_294/pallas_call | solution.py:166
  123.8 3.3 fusion.28
  127.8 2.4 multiply_convert_fusion.11
  131.7 11.7 %collective-permute-done.1 = bf16[128,1792]{1,0:T(8,128)(2,1)S(1)} collective-permute-done((bf16[128,1792]{1,0:T(8,128)(2,1)S(1)}, bf16[128,1792]{1,0:T(8,128)(2,1)S(1)}, u32[]{:S(2)}, u32[]{:S(2)}) %collective-permute-start.1) | collective-permute-done | bytes 458784 | tf_op jit(solution)/shard_map/ppermute | solution.py:66
  144.4 10.8 %collective-permute-done.2 = bf16[128,1792]{1,0:T(8,128)(2,1)S(1)} collective-permute-done((bf16[128,1792]{1,0:T(8,128)(2,1)S(1)}, bf16[128,1792]{1,0:T(8,128)(2,1)S(1)}, u32[]{:S(2)}, u32[]{:S(2)}) %collective-permute-start.2) | collective-permute-done | bytes 458784 | tf_op jit(solution)/shard_map/ppermute | solution.py:66
  155.5 45.8 %all-gather.6.cloned.1.call-done.pooled_ref = bf16[528,128,128]{2,1,0:T(8,128)(2,1)} async-done(((bf16[33,128,128]{2,1,0:T(8,128)(2,1)}), bf16[528,128,128]{2,1,0:T(8,128)(2,1)}) %all-gather.6.cloned.1.call-update) | async-done | bytes 17301520 | tf_op jit(solution)/shard_map/all_gather | solution.py:518
  201.3 20.1 %lay_420.1 = (bf16[3584,128]{1,0:T(8,128)(2,1)}, bf16[5376,896]{1,0:T(8,128)(2,1)}, bf16[896,1792]{1,0:T(8,128)(2,1)}) custom-call(s32[420]{0:T(512)} %slots_ref.9, bf16[528,128,128]{2,1,0:T(8,128)(2,1)} %all-gather.6.cloned.1.call-done.pooled_ref), custom_call_target="tpu_custom_call" | custom-call | bytes 27525120 | tf_op jit(solution)/shard_map/lay_420/pallas_call | solution.py:166
  221.4 3.1 fusion.63
  225.6 3.0 fusion.66
  229.6 3.9 fusion.69
  233.5 2.0 copy.83
  236.5 2.6 fusion.62
  239.1 3.2 fusion.148
  242.3 3.4 fusion.109
  250.6 10.8 %collective-permute-done.3 = bf16[128,1792]{1,0:T(8,128)(2,1)S(1)} collective-permute-done((bf16[128,1792]{1,0:T(8,128)(2,1)S(1)}, bf16[128,1792]{1,0:T(8,128)(2,1)S(1)}, u32[]{:S(2)}, u32[]{:S(2)}) %collective-permute-start.3) | collective-permute-done | bytes 458784 | tf_op jit(solution)/shard_map/ppermute | solution.py:66
  262.2 9.0 collective-permute-done.6
  271.3 9.8 %collective-permute-done.4 = bf16[128,1792]{1,0:T(8,128)(2,1)S(1)} collective-permute-done((bf16[128,1792]{1,0:T(8,128)(2,1)S(1)}, bf16[128,1792]{1,0:T(8,128)(2,1)S(1)}, u32[]{:S(2)}, u32[]{:S(2)}) %collective-permute-start.4) | collective-permute-done | bytes 458784 | tf_op jit(solution)/shard_map/ppermute | solution.py:66
  283.6 84.7 %all-gather.8.cloned.1.call-done.pooled_ref = bf16[1008,128,128]{2,1,0:T(8,128)(2,1)} async-done(((bf16[63,128,128]{2,1,0:T(8,128)(2,1)}), bf16[1008,128,128]{2,1,0:T(8,128)(2,1)}) %all-gather.8.cloned.1.call-update) | async-done | bytes 33030160 | tf_op jit(solution)/shard_map/all_gather | solution.py:518
  368.3 31.9 %lay_798.1 = (bf16[3584,2432]{1,0:T(8,128)(2,1)}, bf16[2432,1792]{1,0:T(8,128)(2,1)}) custom-call(s32[798]{0:T(1024)} %slots_ref.11, bf16[1008,128,128]{2,1,0:T(8,128)(2,1)} %all-gather.8.cloned.1.call-done.pooled_ref), custom_call_target="tpu_custom_call" | custom-call | bytes 52297728 | tf_op jit(solution)/shard_map/lay_798/pallas_call | solution.py:166
  400.3 6.3 fusion.137
  406.7 7.6 fusion.4
  414.3 6.3 multiply_convert_fusion.3
  420.6 26.1 %grad_798.1 = bf16[1008,128,128]{2,1,0:T(8,128)(2,1)} custom-call(s32[798]{0:T(1024)} %slots_ref.11, bf16[256,1792]{1,0:T(8,128)(2,1)} %get-tuple-element.116.refs_0_, bf16[256,2432]{1,0:T(8,128)(2,1)} %get-tuple-element.81.refs_1_, bf16[256,2432]{1,0:T(8,128)(2,1)} %get-tuple-element.83.refs_2_, bf16[256,2432]{1,0:T(8,128)(2,1)} %get-tuple-element.82.refs_3_, ...), custom_call_target="tpu_custom_call" | custom-call | flops 6694109184 | bytes 26148864 | tf_op jit(solution)/shard_map/grad_798/pallas_call | solution.py:255
  446.7 6.5 fusion.2
  453.2 7.1 fusion.45
  462.4 11.8 %collective-permute-done.7 = bf16[128,1792]{1,0:T(8,128)(2,1)S(1)} collective-permute-done((bf16[128,1792]{1,0:T(8,128)(2,1)}, bf16[128,1792]{1,0:T(8,128)(2,1)S(1)}, u32[]{:S(2)}, u32[]{:S(2)}) %collective-permute-start.7) | collective-permute-done | bytes 458784 | tf_op jit(solution)/shard_map/ppermute | solution.py:66
  477.6 10.5 %collective-permute-done.8 = bf16[128,1792]{1,0:T(8,128)(2,1)S(1)} collective-permute-done((bf16[128,1792]{1,0:T(8,128)(2,1)}, bf16[128,1792]{1,0:T(8,128)(2,1)S(1)}, u32[]{:S(2)}, u32[]{:S(2)}) %collective-permute-start.8) | collective-permute-done | bytes 458784 | tf_op jit(solution)/shard_map/ppermute | solution.py:66
  490.2 4.5 convolution_convert_fusion.3
  496.0 3.7 multiply_reduce_fusion
  499.7 4.8 fusion.76
  504.5 5.5 fusion.77
  509.9 2.7 multiply_convert_fusion.5
  526.1 2.5 convolution_convert_fusion
  531.8 2.0 copy.97.refs_6_
  533.8 3.1 collective-permute-done.9
  538.5 8.3 collective-permute-done.5
  546.8 3.5 fusion.145
  556.4 20.2 %grad_420.1 = bf16[528,128,128]{2,1,0:T(8,128)(2,1)} custom-call(s32[420]{0:T(512)} %slots_ref.9, bf16[256,1792]{1,0:T(8,128)(2,1)} %get-tuple-element.112.refs_0_, bf16[256,128]{1,0:T(8,128)(2,1)} %copy.92.refs_1_, bf16[256,128]{1,0:T(8,128)(2,1)} %copy.93.refs_2_, bf16[256,896]{1,0:T(8,128)(2,1)} %copy.94.refs_3_, bf16[256,896]{1,0:T(8,128)(2,1)} %copy.95.refs_4_, ...), custom_call_target="tpu_custom_call" | custom-call | flops 3523215360 | bytes 13762560 | tf_op jit(solution)/shard_map/grad_420/pallas_call | solution.py:255
  578.3 3.5 multiply_reduce_fusion.4
  587.4 14.5 %grad_294.1 = bf16[368,128,128]{2,1,0:T(8,128)(2,1)} custom-call(s32[294]{0:T(512)} %slots_ref.10, bf16[256,1792]{1,0:T(8,128)(2,1)} %get-tuple-element.114.refs_0_, bf16[256,896]{1,0:T(8,128)(2,1)} %copy-done.27, bf16[256,896]{1,0:T(8,128)(2,1)} %copy-done.33, bf16[256,896]{1,0:T(8,128)(2,1)} %copy-done.50, bf16[256,1792]{1,0:T(8,128)(2,1)} %get-tuple-element.115.refs_4_), custom_call_target="tpu_custom_call" | custom-call | flops 2466250752 | bytes 9633792 | tf_op jit(solution)/shard_map/grad_294/pallas_call | solution.py:255
  603.0 271.8 %scatter_sum.1 = (f32[33,128,128]{2,1,0:T(8,128)}, f32[23,128,128]{2,1,0:T(8,128)}, f32[6,1792]{1,0:T(8,128)}) custom-call(bf16[8,2,33,128,128]{4,3,2,1,0:T(8,128)(2,1)} %bitcast.152, bf16[8,2,23,128,128]{4,3,2,1,0:T(8,128)(2,1)} %bitcast.153, f32[6,1792]{1,0:T(8,128)} %pad_maximum_fusion.7.refs_2_), custom_call_target="tpu_custom_call" | custom-call | tf_op jit(solution)/shard_map/scatter_sum/pallas_call | solution.py:445
  877.7 7.7 adam_23.1
  886.1 10.0 %adam_33.1 = f32[3,33,16384]{2,1,0:T(8,128)} custom-call(s32[33,128]{1,0:T(8,128)} %broadcast_in_dim.35.used_ref, f32[3,33,16384]{2,1,0:T(8,128)} %state_ref.4, f32[33,128,128]{2,1,0:T(8,128)} %get-tuple-element.25.summed_ref), custom_call_target="tpu_custom_call" | custom-call | tf_op jit(solution)/shard_map/adam_33/pallas_call | solution.py:501
  897.4 4.1 convert_element_type.335.summed_ref
  902.1 13.5 %adam_63.1 = f32[3,63,16384]{2,1,0:T(8,128)} custom-call(s32[63,128]{1,0:T(8,128)} %broadcast_in_dim.36.used_ref, f32[3,63,16384]{2,1,0:T(8,128)} %state_ref.5, f32[63,128,128]{2,1,0:T(8,128)} %convert_element_type.335.summed_ref), custom_call_target="tpu_custom_call" | custom-call | tf_op jit(solution)/shard_map/adam_63/pallas_call | solution.py:501
  (322 shorter events, 71.1 us)
Async XLA Ops:
  7.2 100.5 %all-gather.4.cloned.1.call-start = ((), (), s32[]{:S(2)}) async-start(), calls=%async_computation.1 | async-start | bytes 12812288 | tf_op jit(solution)/shard_map/all_gather | solution.py:518
  9.9 191.5 %all-gather.6.cloned.1.call-start = ((), (), s32[]{:S(2)}) async-start(), calls=%async_computation.2 | async-start | bytes 18382848 | tf_op jit(solution)/shard_map/all_gather | solution.py:518
  13.2 355.1 %all-gather.8.cloned.1.call-start = ((), (), s32[]{:S(2)}) async-start(), calls=%async_computation.3 | async-start | bytes 35094528 | tf_op jit(solution)/shard_map/all_gather | solution.py:518
  17.8 879.6 %reduce-scatter.4.cloned.1.call-start = ((), (), s32[]{:S(2)}) async-start(), calls=%async_computation.4 | async-start | bytes 35094528
  18.8 104.9 %copy-start.54 = (f32[1792]{0:T(1024)}, f32[1792]{0:T(1024)S(1)}, u32[]{:S(2)}) copy-start(f32[1792]{0:T(1024)S(1)} %get-tuple-element.66) | copy-start | bytes 21508
  19.0 104.8 %copy-start.67 = (f32[128]{0:T(128)}, f32[128]{0:T(128)S(1)}, u32[]{:S(2)}) copy-start(f32[128]{0:T(128)S(1)} %fusion.127) | copy-start | bytes 1540
  19.2 11.6 %collective-permute-start = (bf16[128,1792]{1,0:T(8,128)(2,1)S(1)}, bf16[128,1792]{1,0:T(8,128)(2,1)S(1)}, u32[]{:S(2)}, u32[]{:S(2)}) collective-permute-start(bf16[128,1792]{1,0:T(8,128)(2,1)S(1)} %fusion.92), channel_id=1, source_target_pairs={{0,1},{1,0},{2,3},{3,2},{4,5},{5,4},{6,7},{7,6},{8,9},{9,8},{10,11... | collective-permute-start | bytes 1376264 | tf_op jit(solution)/shard_map/ppermute | solution.py:66
  19.7 107.4 %copy-start.59 = (f32[896]{0:T(1024)}, f32[896]{0:T(1024)S(1)}, u32[]{:S(2)}) copy-start(f32[896]{0:T(1024)S(1)} %get-tuple-element.67) | copy-start | bytes 10756
  19.7 107.4 %copy-start.61 = (f32[896]{0:T(1024)}, f32[896]{0:T(1024)S(1)}, u32[]{:S(2)}) copy-start(f32[896]{0:T(1024)S(1)} %get-tuple-element.68) | copy-start | bytes 10756
  19.7 107.4 %copy-start.63 = (f32[896]{0:T(1024)}, f32[896]{0:T(1024)S(1)}, u32[]{:S(2)}) copy-start(f32[896]{0:T(1024)S(1)} %get-tuple-element.69) | copy-start | bytes 10756
  19.8 107.3 %copy-start.71 = (f32[256]{0:T(256)}, f32[256]{0:T(256)S(1)}, u32[]{:S(2)}) copy-start(f32[256]{0:T(256)S(1)} %get-tuple-element.103) | copy-start | bytes 3076
  19.8 107.4 %copy-start.73 = (f32[256]{0:T(256)}, f32[256]{0:T(256)S(1)}, u32[]{:S(2)}) copy-start(f32[256]{0:T(256)S(1)} %get-tuple-element.104) | copy-start | bytes 3076
  31.1 96.0 %copy-start.13 = (bf16[128,1792]{1,0:T(8,128)(2,1)}, bf16[128,1792]{1,0:T(8,128)(2,1)S(1)}, u32[]{:S(2)}) copy-start(bf16[128,1792]{1,0:T(8,128)(2,1)S(1)} %get-tuple-element.96) | copy-start | bytes 1376260
  31.1 96.0 %copy-start.15 = (bf16[128,1792]{1,0:T(8,128)(2,1)}, bf16[128,1792]{1,0:T(8,128)(2,1)S(1)}, u32[]{:S(2)}) copy-start(bf16[128,1792]{1,0:T(8,128)(2,1)S(1)} %get-tuple-element.97) | copy-start | bytes 1376260
  131.4 12.0 %collective-permute-start.1 = (bf16[128,1792]{1,0:T(8,128)(2,1)S(1)}, bf16[128,1792]{1,0:T(8,128)(2,1)S(1)}, u32[]{:S(2)}, u32[]{:S(2)}) collective-permute-start(bf16[128,1792]{1,0:T(8,128)(2,1)S(1)} %dynamic-slice_bitcast_fusion.5), channel_id=1, source_target_pairs={{0,1},{1,0},{2,3},{3,2},{4,5},{5,4},{6,7},{7,6},{8,9},{9,8},{10,11... | collective-permute-start | bytes 1376264 | tf_op jit(solution)/shard_map/ppermute | solution.py:66
  143.7 77.7 %copy-start.77 = (f32[128]{0:T(128)}, f32[128]{0:T(128)S(1)}, u32[]{:S(2)}) copy-start(f32[128]{0:T(128)S(1)} %get-tuple-element.77) | copy-start | bytes 1540
  143.8 77.6 %copy-start.69 = (f32[128]{0:T(128)}, f32[128]{0:T(128)S(1)}, u32[]{:S(2)}) copy-start(f32[128]{0:T(128)S(1)} %fusion.128) | copy-start | bytes 1540
  143.9 11.3 %collective-permute-start.2 = (bf16[128,1792]{1,0:T(8,128)(2,1)S(1)}, bf16[128,1792]{1,0:T(8,128)(2,1)S(1)}, u32[]{:S(2)}, u32[]{:S(2)}) collective-permute-start(bf16[128,1792]{1,0:T(8,128)(2,1)S(1)} %multiply_convert_fusion.10), channel_id=1, source_target_pairs={{0,1},{1,0},{2,3},{3,2},{4,5},{5,4},{6,7},{7,6},{8,9},{9,8},{10,11... | collective-permute-start | bytes 1376264 | tf_op jit(solution)/shard_map/ppermute | solution.py:66
  144.4 92.1 %copy-start.52 = (f32[256,256]{0,1:T(8,128)}, f32[256,256]{0,1:T(8,128)S(1)}, u32[]{:S(2)}) copy-start(f32[256,256]{0,1:T(8,128)S(1)} %get-tuple-element.102) | copy-start | bytes 786436
  155.5 80.5 %copy-start.17 = (bf16[128,1792]{1,0:T(8,128)(2,1)}, bf16[128,1792]{1,0:T(8,128)(2,1)S(1)}, u32[]{:S(2)}) copy-start(bf16[128,1792]{1,0:T(8,128)(2,1)S(1)} %get-tuple-element.94) | copy-start | bytes 1376260
  155.5 80.5 %copy-start.19 = (bf16[128,1792]{1,0:T(8,128)(2,1)}, bf16[128,1792]{1,0:T(8,128)(2,1)S(1)}, u32[]{:S(2)}) copy-start(bf16[128,1792]{1,0:T(8,128)(2,1)S(1)} %get-tuple-element.95) | copy-start | bytes 1376260
  249.1 12.3 %collective-permute-start.3 = (bf16[128,1792]{1,0:T(8,128)(2,1)S(1)}, bf16[128,1792]{1,0:T(8,128)(2,1)S(1)}, u32[]{:S(2)}, u32[]{:S(2)}) collective-permute-start(bf16[128,1792]{1,0:T(8,128)(2,1)S(1)} %dynamic-slice_bitcast_fusion.4), channel_id=1, source_target_pairs={{0,1},{1,0},{2,3},{3,2},{4,5},{5,4},{6,7},{7,6},{8,9},{9,8},{10,11... | collective-permute-start | bytes 1376264 | tf_op jit(solution)/shard_map/ppermute | solution.py:66
  249.4 21.8 %collective-permute-start.6 = (bf16[128,1792]{1,0:T(8,128)(2,1)S(1)}, bf16[128,1792]{1,0:T(8,128)(2,1)S(1)}, u32[]{:S(2)}, u32[]{:S(2)}) collective-permute-start(bf16[128,1792]{1,0:T(8,128)(2,1)S(1)} %copy-done.1), channel_id=1, source_target_pairs={{0,1},{1,0},{2,3},{3,2},{4,5},{5,4},{6,7},{7,6},{8,9},{9,8},{10,11... | collective-permute-start | bytes 1376264 | tf_op jit(solution)/shard_map/ppermute | solution.py:66
  261.9 19.2 %collective-permute-start.4 = (bf16[128,1792]{1,0:T(8,128)(2,1)S(1)}, bf16[128,1792]{1,0:T(8,128)(2,1)S(1)}, u32[]{:S(2)}, u32[]{:S(2)}) collective-permute-start(bf16[128,1792]{1,0:T(8,128)(2,1)S(1)} %multiply_convert_fusion.9), channel_id=1, source_target_pairs={{0,1},{1,0},{2,3},{3,2},{4,5},{5,4},{6,7},{7,6},{8,9},{9,8},{10,11... | collective-permute-start | bytes 1376264 | tf_op jit(solution)/shard_map/ppermute | solution.py:66
  400.3 14.0 %slice-start.3 = ((s8[17432576]{0:T(1024)(128)(4,1)}), s8[4194304]{0:T(1024)(128)(4,1)S(1)}, s32[]{:S(2)}) async-start(s8[17432576]{0:T(1024)(128)(4,1)} %bitcast.202), calls=%async_computation.8 | async-start | bytes 8388608
  400.3 14.0 %slice-start.4 = ((s8[17432576]{0:T(1024)(128)(4,1)}), s8[4194304]{0:T(1024)(128)(4,1)S(1)}, s32[]{:S(2)}) async-start(s8[17432576]{0:T(1024)(128)(4,1)} %bitcast.202), calls=%async_computation.9 | async-start | bytes 8388608
  400.3 14.0 %slice-start.5 = ((s8[17432576]{0:T(1024)(128)(4,1)}), s8[4194304]{0:T(1024)(128)(4,1)S(1)}, s32[]{:S(2)}) async-start(s8[17432576]{0:T(1024)(128)(4,1)} %bitcast.202), calls=%async_computation.10 | async-start | bytes 8388608
  462.1 12.1 %collective-permute-start.7 = (bf16[128,1792]{1,0:T(8,128)(2,1)}, bf16[128,1792]{1,0:T(8,128)(2,1)S(1)}, u32[]{:S(2)}, u32[]{:S(2)}) collective-permute-start(bf16[128,1792]{1,0:T(8,128)(2,1)} %dynamic-slice_bitcast_fusion.2), channel_id=1, source_target_pairs={{0,1},{1,0},{2,3},{3,2},{4,5},{5,4},{6,7},{7,6},{8,9},{9,8},{10,11... | collective-permute-start | bytes 1376264 | tf_op jit(solution)/shard_map/ppermute | solution.py:66
  462.4 13.4 %copy-start.7 = (bf16[256,1792]{1,0:T(8,128)(2,1)S(1)}, bf16[256,1792]{1,0:T(8,128)(2,1)}, u32[]{:S(2)}) copy-start(bf16[256,1792]{1,0:T(8,128)(2,1)} %copy-done.6) | copy-start | bytes 2752516
  462.4 14.8 %copy-start.57 = (s32[294]{0:T(512)S(1)}, s32[294]{0:T(512)}, u32[]{:S(2)}) copy-start(s32[294]{0:T(512)} %slots_ref.10) | copy-start | bytes 3532
  462.4 15.0 %copy-start.56 = (s32[798]{0:T(1024)S(1)}, s32[798]{0:T(1024)}, u32[]{:S(2)}) copy-start(s32[798]{0:T(1024)} %slots_ref.11) | copy-start | bytes 9580
  476.9 11.2 %collective-permute-start.8 = (bf16[128,1792]{1,0:T(8,128)(2,1)}, bf16[128,1792]{1,0:T(8,128)(2,1)S(1)}, u32[]{:S(2)}, u32[]{:S(2)}) collective-permute-start(bf16[128,1792]{1,0:T(8,128)(2,1)} %fusion.138), channel_id=1, source_target_pairs={{0,1},{1,0},{2,3},{3,2},{4,5},{5,4},{6,7},{7,6},{8,9},{9,8},{10,11... | collective-permute-start | bytes 1376264 | tf_op jit(solution)/shard_map/ppermute | solution.py:66
  525.8 11.1 %collective-permute-start.9 = (bf16[128,1792]{1,0:T(8,128)(2,1)}, bf16[128,1792]{1,0:T(8,128)(2,1)}, u32[]{:S(2)}, u32[]{:S(2)}) collective-permute-start(bf16[128,1792]{1,0:T(8,128)(2,1)} %dynamic-slice_bitcast_fusion.1), channel_id=1, source_target_pairs={{0,1},{1,0},{2,3},{3,2},{4,5},{5,4},{6,7},{7,6},{8,9},{9,8},{10,11... | collective-permute-start | bytes 1376264 | tf_op jit(solution)/shard_map/ppermute | solution.py:66
  530.5 16.3 %collective-permute-start.5 = (bf16[128,1792]{1,0:T(8,128)(2,1)}, bf16[128,1792]{1,0:T(8,128)(2,1)}, u32[]{:S(2)}, u32[]{:S(2)}) collective-permute-start(bf16[128,1792]{1,0:T(8,128)(2,1)} %dynamic-slice_bitcast_fusion.3), channel_id=1, source_target_pairs={{0,1},{1,0},{2,3},{3,2},{4,5},{5,4},{6,7},{7,6},{8,9},{9,8},{10,11... | collective-permute-start | bytes 1376264 | tf_op jit(solution)/shard_map/ppermute | solution.py:66
  533.8 12.9 %copy-start.2 = (bf16[128,1792]{1,0:T(8,128)(2,1)S(1)}, bf16[128,1792]{1,0:T(8,128)(2,1)}, u32[]{:S(2)}) copy-start(bf16[128,1792]{1,0:T(8,128)(2,1)} %param.11) | copy-start | bytes 1376260
  533.8 12.9 %copy-start.4 = (bf16[128,1792]{1,0:T(8,128)(2,1)S(1)}, bf16[128,1792]{1,0:T(8,128)(2,1)}, u32[]{:S(2)}) copy-start(bf16[128,1792]{1,0:T(8,128)(2,1)} %copy-done.3) | copy-start | bytes 1376260
  533.8 12.9 %copy-start.8 = (bf16[256,1792]{1,0:T(8,128)(2,1)S(1)}, bf16[256,1792]{1,0:T(8,128)(2,1)}, u32[]{:S(2)}) copy-start(bf16[256,1792]{1,0:T(8,128)(2,1)} %copy-done.6) | copy-start | bytes 2752516
  538.4 12.2 %copy-start.18 = (bf16[128,1792]{1,0:T(8,128)(2,1)S(1)}, bf16[128,1792]{1,0:T(8,128)(2,1)}, u32[]{:S(2)}) copy-start(bf16[128,1792]{1,0:T(8,128)(2,1)} %copy-done.17) | copy-start | bytes 1376260
  538.4 12.2 %copy-start.20 = (bf16[128,1792]{1,0:T(8,128)(2,1)S(1)}, bf16[128,1792]{1,0:T(8,128)(2,1)}, u32[]{:S(2)}) copy-start(bf16[128,1792]{1,0:T(8,128)(2,1)} %copy-done.19) | copy-start | bytes 1376260
  538.4 12.2 %copy-start.24 = (bf16[128,1792]{1,0:T(8,128)(2,1)S(1)}, bf16[128,1792]{1,0:T(8,128)(2,1)}, u32[]{:S(2)}) copy-start(bf16[128,1792]{1,0:T(8,128)(2,1)} %copy-done.23) | copy-start | bytes 1376260
  550.3 26.5 %collective-permute-start.10 = (bf16[128,1792]{1,0:T(8,128)(2,1)}, bf16[128,1792]{1,0:T(8,128)(2,1)S(1)}, u32[]{:S(2)}, u32[]{:S(2)}) collective-permute-start(bf16[128,1792]{1,0:T(8,128)(2,1)} %get-tuple-element.73), channel_id=1, source_target_pairs={{0,1},{1,0},{2,3},{3,2},{4,5},{5,4},{6,7},{7,6},{8,9},{9,8},{10,11... | collective-permute-start | bytes 1376264 | tf_op jit(solution)/shard_map/ppermute | solution.py:66
  556.4 21.5 %copy-start.39 = (f32[256,896]{1,0:T(8,128)S(1)}, f32[256,896]{1,0:T(8,128)}, u32[]{:S(2)}) copy-start(f32[256,896]{1,0:T(8,128)} %get-tuple-element.105) | copy-start | bytes 2752516
  556.4 21.5 %copy-start.72 = (f32[256]{0:T(256)S(1)}, f32[256]{0:T(256)}, u32[]{:S(2)}) copy-start(f32[256]{0:T(256)} %copy-done.71) | copy-start | bytes 3076
  556.4 21.5 %copy-start.74 = (f32[256]{0:T(256)S(1)}, f32[256]{0:T(256)}, u32[]{:S(2)}) copy-start(f32[256]{0:T(256)} %copy-done.73) | copy-start | bytes 3076
  584.8 17.1 %collective-permute-start.11 = (bf16[128,1792]{1,0:T(8,128)(2,1)S(1)}, bf16[128,1792]{1,0:T(8,128)(2,1)S(1)}, u32[]{:S(2)}, u32[]{:S(2)}) collective-permute-start(bf16[128,1792]{1,0:T(8,128)(2,1)S(1)} %dynamic-slice_bitcast_fusion), channel_id=1, source_target_pairs={{0,1},{1,0},{2,3},{3,2},{4,5},{5,4},{6,7},{7,6},{8,9},{9,8},{10,11... | collective-permute-start | bytes 1376264 | tf_op jit(solution)/shard_map/ppermute | solution.py:66
  587.4 14.5 %copy-start.55 = (f32[1792]{0:T(1024)S(1)}, f32[1792]{0:T(1024)}, u32[]{:S(2)}) copy-start(f32[1792]{0:T(1024)} %copy-done.54) | copy-start | bytes 21508
  587.4 14.6 %copy-start.68 = (f32[128]{0:T(128)S(1)}, f32[128]{0:T(128)}, u32[]{:S(2)}) copy-start(f32[128]{0:T(128)} %copy-done.67) | copy-start | bytes 1540
  603.0 271.8 %copy-start.51 = (f32[3,6,1792]{2,1,0:T(8,128)S(1)}, f32[3,6,1792]{2,1,0:T(8,128)}, u32[]{:S(2)}) copy-start(f32[3,6,1792]{2,1,0:T(8,128)} %param.19) | copy-start | bytes 387076
  (68 other events, 257.1 us)
Sparse Core Ops, SparseCore 0:
  10.8 96.8 all-gather.3
  109.9 91.4 all-gather.5
  202.9 165.3 all-gather.7
  446.8 428.1 reduce-scatter.3
where the time goes:
time: 936 us; the launch traced here: 923 us
  Pallas kernels  432 us (46%)
  waiting for transfers between devices  304 us (32%)
  matrix products  95.9 us (10%)
  other arithmetic  34.6 us (4%)
  local copies, waits for them, and re-layouts  34 us (4%)
  between operations  15.7 us (2%)
    pallas_call x1, Pallas kernels, scatter_sum(): pl.pallas_call(functools.partial(scatter_body, owners, caps, tuple(jobs))...  272 us
    all_gather x3, waiting for transfers between devices, gather_units(): return lax.all_gather(own, 'dp', axis=0, tiled=True)  207 us
    ppermute x12, waiting for transfers between devices, swap(): return lax.ppermute(values, axis, [(i, i ^ bit) for i in range(size)])  96.8 us
    pallas_call x3, Pallas kernels, lay_out(): pl.pallas_call(functools.partial(lay_body, tuple(parts)), grid_spec=pltpu...  68 us
    pallas_call x3, Pallas kernels, grad_units(): pl.pallas_call(functools.partial(grad_body, tuple(parts), len(operands)),...  60.9 us
    dot_general x12, matrix products, product(): return jnp.dot(left, right, preferred_element_type=jnp.float32)  35.3 us
    dot_general x12, matrix products, product_right(): lax.dot_general(left, right, (((1,), (1,)), ((), ())), preferred_element_...  35.1 us
    pallas_call x3, Pallas kernels, adam_units(): pl.pallas_call(functools.partial(adam_body, scale), grid=(unit_width // b...  31.1 us
  transfers between devices with their start and end apart: 16, of which 13 were waited for; matrix products, arithmetic and copies ran while one was open for 14% of the time, Pallas kernels for 39%

commit v1 on v0

--- a/solution.py
+++ b/solution.py
@@ -477,8 +477,11 @@
     return jnp.stack(adam_values(opt_state[0], opt_state[1], opt_state[2], gradient, rate))
 
 
-def adam_body(scale, used_ref, state_ref, summed_ref, out_ref):
+def adam_body(scale, used_ref, state_ref, summed_ref, out_ref, *scratch):
     cap, rows, lanes = summed_ref.shape
+    if scratch:
+        scratch[0][...] = summed_ref[...].astype(jnp.float32)
+        summed_ref = scratch[0]
     flat = summed_ref.reshape(cap * rows, lanes)
     used = used_ref[...] > 0
     for r in range(rows):
@@ -508,14 +511,98 @@
         ],
         out_specs=pl.BlockSpec((3, cap, block), lambda i: (0, 0, i)),
         out_shape=jax.ShapeDtypeStruct(state.shape, jnp.float32),
+        scratch_shapes=[pltpu.VMEM((cap, rows, LANES), jnp.float32)]
+        if summed.dtype == jnp.bfloat16
+        else [],
         name=f"adam_{cap}",
     )(jnp.broadcast_to(used[:, None], (cap, LANES)), state, summed)
 
 
-def gather_units(state, scale):
+def spread_body(owners, cap, jobs, own_ref, out_ref, local_sem, send_sem, recv_sem):
+    stages = bits_of(owners)
+    me = lax.axis_index("dp")
+    ten = lax.axis_index("tensor")
+    bit = [(me // (1 << s)) % 2 for s in range(stages)]
+    partner = [me + (1 - 2 * bit[s]) * (1 << s) for s in range(stages)]
+    barrier = pltpu.get_barrier_semaphore()
+    for s in range(stages):
+        pl.semaphore_signal(barrier, inc=1, device_id=(partner[s], ten), device_id_type=MESH)
+    pl.semaphore_wait(barrier, stages)
+    tail = out_ref.shape[2:]
+
+    def bit_at(s, k):
+        b = stages - 1 - s
+        return 3 - b if jobs[k][2] and b in (1, 2) else b
+
+    def held(s, k):
+        at, size, swapped = jobs[k]
+        span = pl.ds(at, size)
+        b = stages - 1 - s
+        if swapped and b == 2:
+            return out_ref.reshape(owners >> 3, 8, cap, *tail).at[:, me % 8, span]
+        if swapped and b == 1:
+            view = out_ref.reshape(owners >> 3, 2, 2, 2, cap, *tail)
+            return view.at[:, bit[2], :, bit[0], span]
+        low = 1 << (b + 1)
+        return out_ref.reshape(owners // low, low, cap, *tail).at[:, me % low, span]
+
+    def remote(s, k):
+        b = bit_at(s, k)
+        at, size, _ = jobs[k]
+        dst = out_ref.at[me, pl.ds(at, size)] if s == 0 else held(s, k)
+        return pltpu.make_async_remote_copy(
+            src_ref=own_ref.at[pl.ds(at, size)] if s == 0 else dst,
+            dst_ref=dst,
+            send_sem=send_sem.at[s, k],
+            recv_sem=recv_sem.at[s, k],
+            device_id=(partner[b], ten),
+            device_id_type=MESH,
+        )
+
+    local = pltpu.make_async_copy(own_ref, out_ref.at[me], local_sem.at[0])
+    count = len(jobs)
+    for k in range(count):
+        remote(0, k).start()
+    local.start()
+    local.wait()
+    for t in range(count + stages - 1):
+        for s in range(stages):
+            k = t - s
+            if 0 <= k < count:
+                remote(s, k).wait_recv()
+                if s + 1 < stages:
+                    remote(s + 1, k).start()
+    for s in range(stages):
+        for k in range(count):
+            remote(s, k).wait_send()
+
+
+def spread_units(own, owners, collective, most=4):
+    cap, depth, lanes = own.shape
+    stages = bits_of(owners)
+    jobs = tuple(
+        (at, size, stages > 2 and number % 4 == 2)
+        for number, (at, size) in enumerate(chunks_of(cap, most))
+    )
+    out = pl.pallas_call(
+        functools.partial(spread_body, owners, cap, jobs),
+        out_shape=jax.ShapeDtypeStruct((owners, cap, depth, lanes), jnp.bfloat16),
+        in_specs=[pl.BlockSpec(memory_space=pltpu.VMEM)],
+        out_specs=pl.BlockSpec(memory_space=pl.ANY),
+        scratch_shapes=[
+            pltpu.SemaphoreType.DMA((1,)),
+            pltpu.SemaphoreType.DMA((stages, len(jobs))),
+            pltpu.SemaphoreType.DMA((stages, len(jobs))),
+        ],
+        compiler_params=pltpu.CompilerParams(collective_id=collective, has_side_effects=True),
+        name=f"spread_{cap}",
+    )(own)
+    return out.reshape(owners * cap, depth, lanes)
+
+
+def own_units(state, scale):
     cap, unit_width = state.shape[1:]
-    own = (state[0] * scale).reshape(cap, unit_width // LANES, LANES).astype(jnp.bfloat16)
-    return lax.all_gather(own, "dp", axis=0, tiled=True)
+    return (state[0] * scale).reshape(cap, unit_width // LANES, LANES).astype(jnp.bfloat16)
 
 
 def attend(query_f, key_f, query_s, key_s, lin_mask, win_mask):
@@ -557,10 +644,17 @@
     cap_conv = state_conv.shape[1]
     cap_mix = state_mix.shape[1]
     cap_mlp = state_mlp.shape[1]
+    own_conv, own_mix, own_mlp = lax.optimization_barrier(
+        (
+            own_units(state_conv, CONV_SCALE),
+            own_units(state_mix, MIX_SCALE),
+            own_units(state_mlp, MLP_SCALE),
+        )
+    )
     pooled = (
-        gather_units(state_conv, CONV_SCALE),
-        gather_units(state_mix, MIX_SCALE),
-        gather_units(state_mlp, MLP_SCALE),
+        spread_units(own_conv, owners, 2),
+        lax.all_gather(own_mix, "dp", axis=0, tiled=True),
+        lax.all_gather(own_mlp, "dp", axis=0, tiled=True),
     )
     per = D * LANES // unit_width
     narrow, middle = per * feat_cols // LANES, per * half_width // LANES
@@ -652,9 +746,7 @@
             (activated, back_three, LANES),
         ),
     )
-    summed_mlp = lax.psum_scatter(
-        mlp_units, "dp", scatter_dimension=0, tiled=True
-    ).astype(jnp.float32)
+    summed_mlp = lax.psum_scatter(mlp_units, "dp", scatter_dimension=0, tiled=True)
     back_two = gather_rows(back_hidden_two.astype(jnp.bfloat16))
     back_attended = (
         product_right(back_two, mix_w[5]).astype(jnp.bfloat16).reshape(length, local_heads, HEAD)

time: 936 us -> 908 us (0.970)
  the two profiles are of different devices: /device:TPU:15 before, /device:TPU:12 now
where the time goes in v1:
time: 908 us; the launch traced here: 894 us
  Pallas kernels  557 us (61%)
  waiting for transfers between devices  147 us (16%)
  matrix products  95.1 us (10%)
  local copies, waits for them, and re-layouts  34.2 us (4%)
  other arithmetic  30.5 us (3%)
  between operations  15.7 us (2%)
  starting transfers between devices  14.1 us (2%)
    pallas_call x1, Pallas kernels, scatter_sum(): pl.pallas_call(functools.partial(scatter_body, owners, caps, tuple(jobs))...  271 us
    pallas_call x1, Pallas kernels, spread_units(): pl.pallas_call(functools.partial(spread_body, owners, cap, jobs), out_sha...  125 us
    ppermute x12, waiting for transfers between devices, swap(): return lax.ppermute(values, axis, [(i, i ^ bit) for i in range(size)])  84.1 us
    pallas_call x3, Pallas kernels, lay_out(): pl.pallas_call(functools.partial(lay_body, tuple(parts)), grid_spec=pltpu...  67.5 us
    all_gather x1, waiting for transfers between devices, per_device(): lax.all_gather(own_mlp, 'dp', axis=0, tiled=True)  62.4 us
    pallas_call x3, Pallas kernels, grad_units(): pl.pallas_call(functools.partial(grad_body, tuple(parts), len(operands)),...  61.9 us
    dot_general x12, matrix products, product(): return jnp.dot(left, right, preferred_element_type=jnp.float32)  35.4 us
    dot_general x12, matrix products, product_right(): lax.dot_general(left, right, (((1,), (1,)), ((), ())), preferred_element_...  35.2 us
  transfers between devices with their start and end apart: 15, of which 10 were waited for; matrix products, arithmetic and copies ran while one was open for 13% of the time, Pallas kernels for 54%

profile of v1, /device:TPU:12, one launch (start us, length us, event | category | flops | bytes accessed | tf_op | source)
XLA Modules:
  0.0 893.8 jit_solution(10029792474932492925)
XLA Ops:
  9.8 1.9 multiply_convert_fusion.1
  13.1 2.4 multiply_convert_fusion
  20.4 125.4 %spread_23.1 = bf16[16,23,128,128]{3,2,1,0:T(8,128)(2,1)} custom-call(bf16[23,128,128]{2,1,0:T(8,128)(2,1)} %slice.126.own_ref), custom_call_target="tpu_custom_call" | custom-call | tf_op jit(solution)/shard_map/spread_23/pallas_call | solution.py:587
  145.8 16.1 %lay_294.1 = (bf16[3584,896]{1,0:T(8,128)(2,1)}, bf16[896,1792]{1,0:T(8,128)(2,1)}) custom-call(s32[294]{0:T(512)} %slots_ref.10, bf16[368,128,128]{2,1,0:T(8,128)(2,1)} %bitcast.155), custom_call_target="tpu_custom_call" | custom-call | bytes 19267584 | tf_op jit(solution)/shard_map/lay_294/pallas_call | solution.py:166
  162.5 3.4 fusion.28
  166.6 2.4 multiply_convert_fusion.11
  170.2 2.6 collective-permute-start.1
  172.8 11.1 %collective-permute-done.1 = bf16[128,1792]{1,0:T(8,128)(2,1)S(1)} collective-permute-done((bf16[128,1792]{1,0:T(8,128)(2,1)S(1)}, bf16[128,1792]{1,0:T(8,128)(2,1)S(1)}, u32[]{:S(2)}, u32[]{:S(2)}) %collective-permute-start.1) | collective-permute-done | bytes 458784 | tf_op jit(solution)/shard_map/ppermute | solution.py:66
  184.4 1.8 collective-permute-start.2
  186.4 10.5 %collective-permute-done.2 = bf16[128,1792]{1,0:T(8,128)(2,1)S(1)} collective-permute-done((bf16[128,1792]{1,0:T(8,128)(2,1)S(1)}, bf16[128,1792]{1,0:T(8,128)(2,1)S(1)}, u32[]{:S(2)}, u32[]{:S(2)}) %collective-permute-start.2) | collective-permute-done | bytes 458784 | tf_op jit(solution)/shard_map/ppermute | solution.py:66
  197.2 19.6 %lay_420.1 = (bf16[3584,128]{1,0:T(8,128)(2,1)}, bf16[5376,896]{1,0:T(8,128)(2,1)}, bf16[896,1792]{1,0:T(8,128)(2,1)}) custom-call(s32[420]{0:T(512)} %slots_ref.9, bf16[528,128,128]{2,1,0:T(8,128)(2,1)} %all-gather.3.cloned.1.call-done.pooled_ref), custom_call_target="tpu_custom_call" | custom-call | bytes 27525120 | tf_op jit(solution)/shard_map/lay_420/pallas_call | solution.py:166
  216.8 3.1 fusion.63
  220.9 3.0 fusion.66
  224.9 4.0 fusion.69
  228.9 2.1 copy.83
  232.0 2.6 fusion.62
  234.5 3.2 fusion.148
  237.8 3.3 fusion.109
  246.5 11.4 %collective-permute-done.3 = bf16[128,1792]{1,0:T(8,128)(2,1)S(1)} collective-permute-done((bf16[128,1792]{1,0:T(8,128)(2,1)S(1)}, bf16[128,1792]{1,0:T(8,128)(2,1)S(1)}, u32[]{:S(2)}, u32[]{:S(2)}) %collective-permute-start.3) | collective-permute-done | bytes 458784 | tf_op jit(solution)/shard_map/ppermute | solution.py:66
  260.1 7.7 collective-permute-done.6
  267.8 8.0 collective-permute-done.4
  278.4 62.4 %all-gather.5.cloned.1.call-done.pooled_ref = bf16[1008,128,128]{2,1,0:T(8,128)(2,1)} async-done(((bf16[63,128,128]{2,1,0:T(8,128)(2,1)}), bf16[1008,128,128]{2,1,0:T(8,128)(2,1)}) %all-gather.5.cloned.1.call-update) | async-done | bytes 33030160 | tf_op jit(solution)/shard_map/all_gather | solution.py:657
  340.8 31.9 %lay_798.1 = (bf16[3584,2432]{1,0:T(8,128)(2,1)}, bf16[2432,1792]{1,0:T(8,128)(2,1)}) custom-call(s32[798]{0:T(1024)} %slots_ref.11, bf16[1008,128,128]{2,1,0:T(8,128)(2,1)} %all-gather.5.cloned.1.call-done.pooled_ref), custom_call_target="tpu_custom_call" | custom-call | bytes 52297728 | tf_op jit(solution)/shard_map/lay_798/pallas_call | solution.py:166
  372.8 6.3 fusion.137
  379.1 7.6 fusion.4
  386.8 6.3 multiply_convert_fusion.3
  393.1 26.7 %grad_798.1 = bf16[1008,128,128]{2,1,0:T(8,128)(2,1)} custom-call(s32[798]{0:T(1024)} %slots_ref.11, bf16[256,1792]{1,0:T(8,128)(2,1)} %get-tuple-element.122.refs_0_, bf16[256,2432]{1,0:T(8,128)(2,1)} %get-tuple-element.87.refs_1_, bf16[256,2432]{1,0:T(8,128)(2,1)} %get-tuple-element.89.refs_2_, bf16[256,2432]{1,0:T(8,128)(2,1)} %get-tuple-element.88.refs_3_, ...), custom_call_target="tpu_custom_call" | custom-call | flops 6694109184 | bytes 26148864 | tf_op jit(solution)/shard_map/grad_798/pallas_call | solution.py:255
  419.8 6.5 fusion.2
  426.4 7.2 fusion.45
  435.8 12.5 %collective-permute-done.7 = bf16[128,1792]{1,0:T(8,128)(2,1)S(1)} collective-permute-done((bf16[128,1792]{1,0:T(8,128)(2,1)}, bf16[128,1792]{1,0:T(8,128)(2,1)S(1)}, u32[]{:S(2)}, u32[]{:S(2)}) %collective-permute-start.7) | collective-permute-done | bytes 458784 | tf_op jit(solution)/shard_map/ppermute | solution.py:66
  451.9 11.2 %collective-permute-done.8 = bf16[128,1792]{1,0:T(8,128)(2,1)S(1)} collective-permute-done((bf16[128,1792]{1,0:T(8,128)(2,1)}, bf16[128,1792]{1,0:T(8,128)(2,1)S(1)}, u32[]{:S(2)}, u32[]{:S(2)}) %collective-permute-start.8) | collective-permute-done | bytes 458784 | tf_op jit(solution)/shard_map/ppermute | solution.py:66
  465.2 4.6 convolution_convert_fusion.3
  471.0 3.6 multiply_reduce_fusion
  474.6 4.8 fusion.76
  479.4 4.8 fusion.77
  484.2 2.7 multiply_convert_fusion.5
  500.6 2.5 convolution_convert_fusion
  506.6 2.1 copy.97.refs_6_
  508.7 5.0 collective-permute-done.9
  515.3 6.7 collective-permute-done.5
  521.9 3.4 fusion.145
  531.8 20.7 %grad_420.1 = bf16[528,128,128]{2,1,0:T(8,128)(2,1)} custom-call(s32[420]{0:T(512)} %slots_ref.9, bf16[256,1792]{1,0:T(8,128)(2,1)} %get-tuple-element.118.refs_0_, bf16[256,128]{1,0:T(8,128)(2,1)} %copy.92.refs_1_, bf16[256,128]{1,0:T(8,128)(2,1)} %copy.93.refs_2_, bf16[256,896]{1,0:T(8,128)(2,1)} %copy.94.refs_3_, bf16[256,896]{1,0:T(8,128)(2,1)} %copy.95.refs_4_, ...), custom_call_target="tpu_custom_call" | custom-call | flops 3523215360 | bytes 13762560 | tf_op jit(solution)/shard_map/grad_420/pallas_call | solution.py:255
  554.0 3.6 multiply_reduce_fusion.4
  563.5 14.5 %grad_294.1 = bf16[368,128,128]{2,1,0:T(8,128)(2,1)} custom-call(s32[294]{0:T(512)} %slots_ref.10, bf16[256,1792]{1,0:T(8,128)(2,1)} %get-tuple-element.120.refs_0_, bf16[256,896]{1,0:T(8,128)(2,1)} %copy-done.27, bf16[256,896]{1,0:T(8,128)(2,1)} %copy-done.33, bf16[256,896]{1,0:T(8,128)(2,1)} %copy-done.50, bf16[256,1792]{1,0:T(8,128)(2,1)} %get-tuple-element.121.refs_4_), custom_call_target="tpu_custom_call" | custom-call | flops 2466250752 | bytes 9633792 | tf_op jit(solution)/shard_map/grad_294/pallas_call | solution.py:255
  579.2 270.6 %scatter_sum.1 = (f32[33,128,128]{2,1,0:T(8,128)}, f32[23,128,128]{2,1,0:T(8,128)}, f32[6,1792]{1,0:T(8,128)}) custom-call(bf16[8,2,33,128,128]{4,3,2,1,0:T(8,128)(2,1)} %bitcast.153, bf16[8,2,23,128,128]{4,3,2,1,0:T(8,128)(2,1)} %bitcast.154, f32[6,1792]{1,0:T(8,128)} %pad_maximum_fusion.7.refs_2_), custom_call_target="tpu_custom_call" | custom-call | tf_op jit(solution)/shard_map/scatter_sum/pallas_call | solution.py:445
  852.7 7.7 adam_23.1
  861.1 10.0 %adam_33.1 = f32[3,33,16384]{2,1,0:T(8,128)} custom-call(s32[33,128]{1,0:T(8,128)} %broadcast_in_dim.35.used_ref, f32[3,33,16384]{2,1,0:T(8,128)} %state_ref.4, f32[33,128,128]{2,1,0:T(8,128)} %get-tuple-element.31.summed_ref), custom_call_target="tpu_custom_call" | custom-call | tf_op jit(solution)/shard_map/adam_33/pallas_call | solution.py:504
  873.0 13.8 %adam_63.1 = f32[3,63,16384]{2,1,0:T(8,128)} custom-call(s32[63,128]{1,0:T(8,128)} %broadcast_in_dim.36.used_ref, f32[3,63,16384]{2,1,0:T(8,128)} %state_ref.5, bf16[63,128,128]{2,1,0:T(8,128)(2,1)} %reduce-scatter.4.cloned.1.call-done.summed_ref), custom_call_target="tpu_custom_call" | custom-call | tf_op jit(solution)/shard_map/adam_63/pallas_call | solution.py:504
  (319 shorter events, 73.0 us)
Async XLA Ops:
  7.2 190.1 %all-gather.3.cloned.1.call-start = ((), (), s32[]{:S(2)}) async-start(), calls=%async_computation.1 | async-start | bytes 18382848 | tf_op jit(solution)/shard_map/all_gather | solution.py:656
  17.7 323.2 %all-gather.5.cloned.1.call-start = ((), (), s32[]{:S(2)}) async-start(), calls=%async_computation.2 | async-start | bytes 35094528 | tf_op jit(solution)/shard_map/all_gather | solution.py:657
  18.4 853.9 %reduce-scatter.4.cloned.1.call-start = ((), (), s32[]{:S(2)}) async-start(), calls=%async_computation.3 | async-start | bytes 35094528
  19.4 142.8 %copy-start.54 = (f32[1792]{0:T(1024)}, f32[1792]{0:T(1024)S(1)}, u32[]{:S(2)}) copy-start(f32[1792]{0:T(1024)S(1)} %get-tuple-element.72) | copy-start | bytes 21508
  19.6 126.3 %copy-start.75 = (f32[128]{0:T(128)}, f32[128]{0:T(128)S(1)}, u32[]{:S(2)}) copy-start(f32[128]{0:T(128)S(1)} %fusion.97) | copy-start | bytes 1540
  19.6 142.6 %copy-start.67 = (f32[128]{0:T(128)}, f32[128]{0:T(128)S(1)}, u32[]{:S(2)}) copy-start(f32[128]{0:T(128)S(1)} %fusion.127) | copy-start | bytes 1540
  19.8 142.4 %collective-permute-start = (bf16[128,1792]{1,0:T(8,128)(2,1)S(1)}, bf16[128,1792]{1,0:T(8,128)(2,1)S(1)}, u32[]{:S(2)}, u32[]{:S(2)}) collective-permute-start(bf16[128,1792]{1,0:T(8,128)(2,1)S(1)} %fusion.92), channel_id=1, source_target_pairs={{0,1},{1,0},{2,3},{3,2},{4,5},{5,4},{6,7},{7,6},{8,9},{9,8},{10,11... | collective-permute-start | bytes 1376264 | tf_op jit(solution)/shard_map/ppermute | solution.py:66
  145.8 16.2 %copy-start.65 = (s32[1,256]{1,0:T(1,128)S(1)}, s32[1,256]{1,0:T(1,128)}, u32[]{:S(2)}) copy-start(s32[1,256]{1,0:T(1,128)} %param.12) | copy-start | bytes 3076
  170.2 13.7 %collective-permute-start.1 = (bf16[128,1792]{1,0:T(8,128)(2,1)S(1)}, bf16[128,1792]{1,0:T(8,128)(2,1)S(1)}, u32[]{:S(2)}, u32[]{:S(2)}) collective-permute-start(bf16[128,1792]{1,0:T(8,128)(2,1)S(1)} %dynamic-slice_bitcast_fusion.5), channel_id=1, source_target_pairs={{0,1},{1,0},{2,3},{3,2},{4,5},{5,4},{6,7},{7,6},{8,9},{9,8},{10,11... | collective-permute-start | bytes 1376264 | tf_op jit(solution)/shard_map/ppermute | solution.py:66
  184.3 32.5 %copy-start.77 = (f32[128]{0:T(128)}, f32[128]{0:T(128)S(1)}, u32[]{:S(2)}) copy-start(f32[128]{0:T(128)S(1)} %get-tuple-element.83) | copy-start | bytes 1540
  184.3 32.5 %copy-start.69 = (f32[128]{0:T(128)}, f32[128]{0:T(128)S(1)}, u32[]{:S(2)}) copy-start(f32[128]{0:T(128)S(1)} %fusion.128) | copy-start | bytes 1540
  184.4 12.5 %collective-permute-start.2 = (bf16[128,1792]{1,0:T(8,128)(2,1)S(1)}, bf16[128,1792]{1,0:T(8,128)(2,1)S(1)}, u32[]{:S(2)}, u32[]{:S(2)}) collective-permute-start(bf16[128,1792]{1,0:T(8,128)(2,1)S(1)} %multiply_convert_fusion.10), channel_id=1, source_target_pairs={{0,1},{1,0},{2,3},{3,2},{4,5},{5,4},{6,7},{7,6},{8,9},{9,8},{10,11... | collective-permute-start | bytes 1376264 | tf_op jit(solution)/shard_map/ppermute | solution.py:66
  186.4 45.6 %copy-start.52 = (f32[256,256]{0,1:T(8,128)}, f32[256,256]{0,1:T(8,128)S(1)}, u32[]{:S(2)}) copy-start(f32[256,256]{0,1:T(8,128)S(1)} %get-tuple-element.108) | copy-start | bytes 786436
  197.2 34.3 %copy-start.17 = (bf16[128,1792]{1,0:T(8,128)(2,1)}, bf16[128,1792]{1,0:T(8,128)(2,1)S(1)}, u32[]{:S(2)}) copy-start(bf16[128,1792]{1,0:T(8,128)(2,1)S(1)} %get-tuple-element.100) | copy-start | bytes 1376260
  197.2 34.3 %copy-start.19 = (bf16[128,1792]{1,0:T(8,128)(2,1)}, bf16[128,1792]{1,0:T(8,128)(2,1)S(1)}, u32[]{:S(2)}) copy-start(bf16[128,1792]{1,0:T(8,128)(2,1)S(1)} %get-tuple-element.101) | copy-start | bytes 1376260
  244.4 13.5 %collective-permute-start.3 = (bf16[128,1792]{1,0:T(8,128)(2,1)S(1)}, bf16[128,1792]{1,0:T(8,128)(2,1)S(1)}, u32[]{:S(2)}, u32[]{:S(2)}) collective-permute-start(bf16[128,1792]{1,0:T(8,128)(2,1)S(1)} %dynamic-slice_bitcast_fusion.4), channel_id=1, source_target_pairs={{0,1},{1,0},{2,3},{3,2},{4,5},{5,4},{6,7},{7,6},{8,9},{9,8},{10,11... | collective-permute-start | bytes 1376264 | tf_op jit(solution)/shard_map/ppermute | solution.py:66
  246.2 21.6 %collective-permute-start.6 = (bf16[128,1792]{1,0:T(8,128)(2,1)S(1)}, bf16[128,1792]{1,0:T(8,128)(2,1)S(1)}, u32[]{:S(2)}, u32[]{:S(2)}) collective-permute-start(bf16[128,1792]{1,0:T(8,128)(2,1)S(1)} %copy-done.1), channel_id=1, source_target_pairs={{0,1},{1,0},{2,3},{3,2},{4,5},{5,4},{6,7},{7,6},{8,9},{9,8},{10,11... | collective-permute-start | bytes 1376264 | tf_op jit(solution)/shard_map/ppermute | solution.py:66
  258.4 17.5 %collective-permute-start.4 = (bf16[128,1792]{1,0:T(8,128)(2,1)S(1)}, bf16[128,1792]{1,0:T(8,128)(2,1)S(1)}, u32[]{:S(2)}, u32[]{:S(2)}) collective-permute-start(bf16[128,1792]{1,0:T(8,128)(2,1)S(1)} %multiply_convert_fusion.9), channel_id=1, source_target_pairs={{0,1},{1,0},{2,3},{3,2},{4,5},{5,4},{6,7},{7,6},{8,9},{9,8},{10,11... | collective-permute-start | bytes 1376264 | tf_op jit(solution)/shard_map/ppermute | solution.py:66
  372.7 14.0 %slice-start.3 = ((s8[17432576]{0:T(1024)(128)(4,1)}), s8[4194304]{0:T(1024)(128)(4,1)S(1)}, s32[]{:S(2)}) async-start(s8[17432576]{0:T(1024)(128)(4,1)} %bitcast.204), calls=%async_computation.7 | async-start | bytes 8388608
  372.8 14.0 %slice-start.4 = ((s8[17432576]{0:T(1024)(128)(4,1)}), s8[4194304]{0:T(1024)(128)(4,1)S(1)}, s32[]{:S(2)}) async-start(s8[17432576]{0:T(1024)(128)(4,1)} %bitcast.204), calls=%async_computation.8 | async-start | bytes 8388608
  372.8 14.0 %slice-start.5 = ((s8[17432576]{0:T(1024)(128)(4,1)}), s8[4194304]{0:T(1024)(128)(4,1)S(1)}, s32[]{:S(2)}) async-start(s8[17432576]{0:T(1024)(128)(4,1)} %bitcast.204), calls=%async_computation.9 | async-start | bytes 8388608
  435.3 13.0 %collective-permute-start.7 = (bf16[128,1792]{1,0:T(8,128)(2,1)}, bf16[128,1792]{1,0:T(8,128)(2,1)S(1)}, u32[]{:S(2)}, u32[]{:S(2)}) collective-permute-start(bf16[128,1792]{1,0:T(8,128)(2,1)} %dynamic-slice_bitcast_fusion.2), channel_id=1, source_target_pairs={{0,1},{1,0},{2,3},{3,2},{4,5},{5,4},{6,7},{7,6},{8,9},{9,8},{10,11... | collective-permute-start | bytes 1376264 | tf_op jit(solution)/shard_map/ppermute | solution.py:66
  435.8 14.0 %copy-start.7 = (bf16[256,1792]{1,0:T(8,128)(2,1)S(1)}, bf16[256,1792]{1,0:T(8,128)(2,1)}, u32[]{:S(2)}) copy-start(bf16[256,1792]{1,0:T(8,128)(2,1)} %copy-done.6) | copy-start | bytes 2752516
  435.8 15.7 %copy-start.57 = (s32[294]{0:T(512)S(1)}, s32[294]{0:T(512)}, u32[]{:S(2)}) copy-start(s32[294]{0:T(512)} %slots_ref.10) | copy-start | bytes 3532
  435.8 15.9 %copy-start.56 = (s32[798]{0:T(1024)S(1)}, s32[798]{0:T(1024)}, u32[]{:S(2)}) copy-start(s32[798]{0:T(1024)} %slots_ref.11) | copy-start | bytes 9580
  451.0 12.1 %collective-permute-start.8 = (bf16[128,1792]{1,0:T(8,128)(2,1)}, bf16[128,1792]{1,0:T(8,128)(2,1)S(1)}, u32[]{:S(2)}, u32[]{:S(2)}) collective-permute-start(bf16[128,1792]{1,0:T(8,128)(2,1)} %fusion.138), channel_id=1, source_target_pairs={{0,1},{1,0},{2,3},{3,2},{4,5},{5,4},{6,7},{7,6},{8,9},{9,8},{10,11... | collective-permute-start | bytes 1376264 | tf_op jit(solution)/shard_map/ppermute | solution.py:66
  492.1 8.5 slice-start.8
  500.0 13.7 %copy-start.70 = (f32[128]{0:T(128)S(1)}, f32[128]{0:T(128)}, u32[]{:S(2)}) copy-start(f32[128]{0:T(128)} %copy-done.69) | copy-start | bytes 1540
  500.0 13.7 %collective-permute-start.9 = (bf16[128,1792]{1,0:T(8,128)(2,1)}, bf16[128,1792]{1,0:T(8,128)(2,1)}, u32[]{:S(2)}, u32[]{:S(2)}) collective-permute-start(bf16[128,1792]{1,0:T(8,128)(2,1)} %dynamic-slice_bitcast_fusion.1), channel_id=1, source_target_pairs={{0,1},{1,0},{2,3},{3,2},{4,5},{5,4},{6,7},{7,6},{8,9},{9,8},{10,11... | collective-permute-start | bytes 1376264 | tf_op jit(solution)/shard_map/ppermute | solution.py:66
  503.1 12.1 %copy-start.78 = (f32[128]{0:T(128)S(1)}, f32[128]{0:T(128)}, u32[]{:S(2)}) copy-start(f32[128]{0:T(128)} %copy-done.77) | copy-start | bytes 1540
  504.9 17.0 %collective-permute-start.5 = (bf16[128,1792]{1,0:T(8,128)(2,1)}, bf16[128,1792]{1,0:T(8,128)(2,1)}, u32[]{:S(2)}, u32[]{:S(2)}) collective-permute-start(bf16[128,1792]{1,0:T(8,128)(2,1)} %dynamic-slice_bitcast_fusion.3), channel_id=1, source_target_pairs={{0,1},{1,0},{2,3},{3,2},{4,5},{5,4},{6,7},{7,6},{8,9},{9,8},{10,11... | collective-permute-start | bytes 1376264 | tf_op jit(solution)/shard_map/ppermute | solution.py:66
  508.7 13.2 %copy-start.2 = (bf16[128,1792]{1,0:T(8,128)(2,1)S(1)}, bf16[128,1792]{1,0:T(8,128)(2,1)}, u32[]{:S(2)}) copy-start(bf16[128,1792]{1,0:T(8,128)(2,1)} %param.11) | copy-start | bytes 1376260
  508.7 13.2 %copy-start.4 = (bf16[128,1792]{1,0:T(8,128)(2,1)S(1)}, bf16[128,1792]{1,0:T(8,128)(2,1)}, u32[]{:S(2)}) copy-start(bf16[128,1792]{1,0:T(8,128)(2,1)} %copy-done.3) | copy-start | bytes 1376260
  508.7 13.2 %copy-start.8 = (bf16[256,1792]{1,0:T(8,128)(2,1)S(1)}, bf16[256,1792]{1,0:T(8,128)(2,1)}, u32[]{:S(2)}) copy-start(bf16[256,1792]{1,0:T(8,128)(2,1)} %copy-done.6) | copy-start | bytes 2752516
  515.2 10.7 %copy-start.18 = (bf16[128,1792]{1,0:T(8,128)(2,1)S(1)}, bf16[128,1792]{1,0:T(8,128)(2,1)}, u32[]{:S(2)}) copy-start(bf16[128,1792]{1,0:T(8,128)(2,1)} %copy-done.17) | copy-start | bytes 1376260
  515.2 10.7 %copy-start.20 = (bf16[128,1792]{1,0:T(8,128)(2,1)S(1)}, bf16[128,1792]{1,0:T(8,128)(2,1)}, u32[]{:S(2)}) copy-start(bf16[128,1792]{1,0:T(8,128)(2,1)} %copy-done.19) | copy-start | bytes 1376260
  515.2 10.7 %copy-start.24 = (bf16[128,1792]{1,0:T(8,128)(2,1)S(1)}, bf16[128,1792]{1,0:T(8,128)(2,1)}, u32[]{:S(2)}) copy-start(bf16[128,1792]{1,0:T(8,128)(2,1)} %copy-done.23) | copy-start | bytes 1376260
  515.3 10.7 %copy-start.26 = (bf16[128,1792]{1,0:T(8,128)(2,1)S(1)}, bf16[128,1792]{1,0:T(8,128)(2,1)}, u32[]{:S(2)}) copy-start(bf16[128,1792]{1,0:T(8,128)(2,1)} %copy-done.25) | copy-start | bytes 1376260
  525.4 27.1 %collective-permute-start.10 = (bf16[128,1792]{1,0:T(8,128)(2,1)}, bf16[128,1792]{1,0:T(8,128)(2,1)S(1)}, u32[]{:S(2)}, u32[]{:S(2)}) collective-permute-start(bf16[128,1792]{1,0:T(8,128)(2,1)} %get-tuple-element.79), channel_id=1, source_target_pairs={{0,1},{1,0},{2,3},{3,2},{4,5},{5,4},{6,7},{7,6},{8,9},{9,8},{10,11... | collective-permute-start | bytes 1376264 | tf_op jit(solution)/shard_map/ppermute | solution.py:66
  531.8 21.9 %copy-start.39 = (f32[256,896]{1,0:T(8,128)S(1)}, f32[256,896]{1,0:T(8,128)}, u32[]{:S(2)}) copy-start(f32[256,896]{1,0:T(8,128)} %get-tuple-element.111) | copy-start | bytes 2752516
  531.8 21.9 %copy-start.72 = (f32[256]{0:T(256)S(1)}, f32[256]{0:T(256)}, u32[]{:S(2)}) copy-start(f32[256]{0:T(256)} %copy-done.71) | copy-start | bytes 3076
  531.8 22.0 %copy-start.74 = (f32[256]{0:T(256)S(1)}, f32[256]{0:T(256)}, u32[]{:S(2)}) copy-start(f32[256]{0:T(256)} %copy-done.73) | copy-start | bytes 3076
  560.5 17.5 %collective-permute-start.11 = (bf16[128,1792]{1,0:T(8,128)(2,1)S(1)}, bf16[128,1792]{1,0:T(8,128)(2,1)S(1)}, u32[]{:S(2)}, u32[]{:S(2)}) collective-permute-start(bf16[128,1792]{1,0:T(8,128)(2,1)S(1)} %dynamic-slice_bitcast_fusion), channel_id=1, source_target_pairs={{0,1},{1,0},{2,3},{3,2},{4,5},{5,4},{6,7},{7,6},{8,9},{9,8},{10,11... | collective-permute-start | bytes 1376264 | tf_op jit(solution)/shard_map/ppermute | solution.py:66
  563.5 14.6 %copy-start.55 = (f32[1792]{0:T(1024)S(1)}, f32[1792]{0:T(1024)}, u32[]{:S(2)}) copy-start(f32[1792]{0:T(1024)} %copy-done.54) | copy-start | bytes 21508
  563.5 14.6 %copy-start.68 = (f32[128]{0:T(128)S(1)}, f32[128]{0:T(128)}, u32[]{:S(2)}) copy-start(f32[128]{0:T(128)} %copy-done.67) | copy-start | bytes 1540
  579.2 270.6 %copy-start.51 = (f32[3,6,1792]{2,1,0:T(8,128)S(1)}, f32[3,6,1792]{2,1,0:T(8,128)}, u32[]{:S(2)}) copy-start(f32[3,6,1792]{2,1,0:T(8,128)} %param.19) | copy-start | bytes 387076
  861.1 10.0 %copy-start.76 = (f32[128]{0:T(128)S(1)}, f32[128]{0:T(128)}, u32[]{:S(2)}) copy-start(f32[128]{0:T(128)} %copy-done.75) | copy-start | bytes 1540
  861.1 10.0 %copy-start.5 = (f32[128,1792]{1,0:T(8,128)S(1)}, f32[128,1792]{1,0:T(8,128)}, u32[]{:S(2)}) copy-start(f32[128,1792]{1,0:T(8,128)} %get-tuple-element.80) | copy-start | bytes 2752516
  (67 other events, 222.0 us)
Sparse Core Ops, SparseCore 0:
  17.8 143.7 all-gather.2
  163.1 177.6 all-gather.4
  419.9 428.8 reduce-scatter.3

commit v2 on v1

--- a/solution.py
+++ b/solution.py
@@ -182,6 +182,137 @@
         ),
         name=f"lay_{first}",
     )(slots, pooled)
+
+
+def ffn_body(wide, slots_ref, pooled_ref, u_ref, y_ref, *refs):
+    out_ref, hid_ref, dgt_ref, dup_ref, du_ref = refs[:5]
+    first_w, last_w, buf, stage, sem = refs[5:]
+    depth = buf.shape[2]
+    width, model = u_ref.shape[1], last_w.shape[1]
+    hidden = last_w.shape[0]
+    ring = buf.shape[0]
+    kinds = (
+        (0, 2 * wide, hidden // LANES, 1, first_w),
+        (2 * wide, wide, model // LANES // 2, 2, last_w),
+    )
+    steps = [kind[1] // (kind[2] * kind[3]) for kind in kinds]
+    total = sum(steps)
+
+    def fetch(at):
+        for p, (first, _, nu, blocks, _) in enumerate(kinds):
+            begin = sum(steps[:p])
+
+            @pl.when((at >= begin) & (at < begin + steps[p]))
+            def _():
+                for q in range(nu * blocks):
+                    unit = first + (at - begin) * (nu * blocks) + q
+                    pltpu.make_async_copy(
+                        pooled_ref.at[slots_ref[unit]], buf.at[at % ring, q], sem.at[at % ring]
+                    ).start()
+
+    for at in range(ring - 1):
+        fetch(jnp.int32(at))
+    for p, (first, _, nu, blocks, into) in enumerate(kinds):
+        begin = sum(steps[:p])
+        m = into.shape[1] // LANES
+        rows = nu * depth // m
+
+        def step_of(step, carry):
+            at = begin + step
+            half = at % ring
+            fetch(at + ring - 1)
+            pltpu.make_async_copy(
+                pooled_ref.at[pl.ds(0, nu * blocks)], buf.at[half, pl.ds(0, nu * blocks)], sem.at[half]
+            ).wait()
+            for block in range(blocks):
+                for q in range(nu):
+                    stage[q * depth : (q + 1) * depth, :] = buf[half, block * nu + q].astype(
+                        jnp.float32
+                    )
+                row = pl.multiple_of(step * (rows * blocks) + block * rows, rows)
+                for c in range(m):
+                    into[pl.ds(row, rows), c * LANES : (c + 1) * LANES] = stage[
+                        pl.ds(c, rows, stride=m), :
+                    ].astype(jnp.bfloat16)
+            return carry
+
+        lax.fori_loop(0, steps[p], step_of, 0)
+
+    def hidden_columns(at, size):
+        span = pl.ds(at, size)
+        gate = jnp.dot(u_ref[...], first_w[:width, span], preferred_element_type=jnp.float32)
+        up = jnp.dot(u_ref[...], first_w[width:, span], preferred_element_type=jnp.float32)
+        back = lax.dot_general(
+            y_ref[...], last_w[span, :], (((1,), (1,)), ((), ())), preferred_element_type=jnp.float32
+        )
+        sig = jax.nn.sigmoid(gate)
+        hid_ref[:, span] = (gate * sig * up).astype(jnp.bfloat16)
+        dgt_ref[:, span] = (back * up * sig * (1.0 + gate * (1.0 - sig))).astype(jnp.bfloat16)
+        dup_ref[:, span] = (back * gate * sig).astype(jnp.bfloat16)
+
+    block = 2 * LANES
+
+    def over(extent, run):
+        def body(j, carry):
+            run(pl.multiple_of(j * block, block), block)
+            return carry
+
+        lax.fori_loop(0, extent // block, body, 0)
+        if extent % block:
+            run(extent - extent % block, extent % block)
+
+    over(hidden, hidden_columns)
+
+    def model_columns(at, size):
+        span = pl.ds(at, size)
+        back = lax.dot_general(
+            dgt_ref[...], first_w[span, :], (((1,), (1,)), ((), ())), preferred_element_type=jnp.float32
+        ) + lax.dot_general(
+            dup_ref[...],
+            first_w[pl.ds(width + at, size), :],
+            (((1,), (1,)), ((), ())),
+            preferred_element_type=jnp.float32,
+        )
+        du_ref[:, span] = back.astype(jnp.bfloat16)
+        out_ref[:, span] = jnp.dot(
+            hid_ref[...], last_w[:, span], preferred_element_type=jnp.float32
+        ).astype(jnp.bfloat16)
+
+    over(model, model_columns)
+
+
+def feed_forward(pooled, slots, wide, u, y, hidden):
+    tokens, model = u.shape
+    depth = pooled.shape[1]
+    small = jax.ShapeDtypeStruct((tokens, model), jnp.bfloat16)
+    large = jax.ShapeDtypeStruct((tokens, hidden), jnp.bfloat16)
+    nu = max(hidden // LANES, model // LANES)
+    return pl.pallas_call(
+        functools.partial(ffn_body, wide),
+        grid_spec=pltpu.PrefetchScalarGridSpec(
+            num_scalar_prefetch=1,
+            in_specs=[
+                pl.BlockSpec(memory_space=pl.ANY),
+                pl.BlockSpec(memory_space=pltpu.VMEM),
+                pl.BlockSpec(memory_space=pltpu.VMEM),
+            ],
+            out_specs=[pl.BlockSpec(memory_space=pltpu.VMEM)] * 5,
+            scratch_shapes=[
+                pltpu.VMEM((2 * model, hidden), jnp.bfloat16),
+                pltpu.VMEM((hidden, model), jnp.bfloat16),
+                pltpu.VMEM((4, nu, depth, LANES), jnp.bfloat16),
+                pltpu.VMEM((nu * depth, LANES), jnp.float32),
+                pltpu.SemaphoreType.DMA((4,)),
+            ],
+        ),
+        out_shape=[small, large, large, large, small],
+        cost_estimate=pl.CostEstimate(
+            flops=12 * tokens * model * hidden,
+            bytes_accessed=6 * model * hidden,
+            transcendentals=tokens * hidden,
+        ),
+        name="feed_forward",
+    )(slots, pooled, u, y)
 
 
 def grad_body(parts, sources, slots_ref, *refs):
@@ -676,10 +807,6 @@
         mix_trio[2 * D :],
         mix_back,
     ]
-    mlp_pair, mlp_back = lay_out(
-        pooled[2], slot_mlp, ((2 * wide, ff_half, 19, 2), (wide, D, 7, 2))
-    )
-    mlp_w = [mlp_pair[:D], mlp_pair[D:], mlp_back]
     params = small_state[0] * SMALL_SCALE
     seg_ids = segments[0]
     length = seg_ids.shape[0]
@@ -721,22 +848,11 @@
     hidden_two = hidden_one + sum_rows(product(mix_out, mix_w[5]))
     normed_three = norm_rows(hidden_two, params[2]).astype(jnp.bfloat16)
     ff_in = gather_rows(normed_three)
-    gate_proj = product(ff_in, mlp_w[0])
-    up_proj = product(ff_in, mlp_w[1])
-    activated = (jax.nn.silu(gate_proj) * up_proj).astype(jnp.bfloat16)
-    result = (hidden_two + sum_rows(product(activated, mlp_w[2]))).astype(jnp.bfloat16)
     back_three = gather_rows(cotangent)
-    back_act = product_right(back_three, mlp_w[2])
-    gate_sig = jax.nn.sigmoid(gate_proj)
-    back_gate = (back_act * up_proj * gate_sig * (1.0 + gate_proj * (1.0 - gate_sig))).astype(
-        jnp.bfloat16
-    )
-    back_up = (back_act * gate_proj * gate_sig).astype(jnp.bfloat16)
-    back_normed_three = sum_rows(
-        product_right(back_gate, mlp_w[0]) + product_right(back_up, mlp_w[1])
-    )
-    back_norm_three, gain_three = norm_back(hidden_two, params[2], back_normed_three)
-    back_hidden_two = cotangent.astype(jnp.float32) + back_norm_three
+    part_out, activated, back_gate, back_up, part_back = feed_forward(
+        pooled[2], slot_mlp, wide, ff_in, back_three, ff_half
+    )
+    back_normed_three = sum_rows(part_back)
     mlp_units = grad_units(
         owners * cap_mlp,
         slot_mlp,
@@ -747,6 +863,9 @@
         ),
     )
     summed_mlp = lax.psum_scatter(mlp_units, "dp", scatter_dimension=0, tiled=True)
+    result = (hidden_two + sum_rows(part_out)).astype(jnp.bfloat16)
+    back_norm_three, gain_three = norm_back(hidden_two, params[2], back_normed_three)
+    back_hidden_two = cotangent.astype(jnp.float32) + back_norm_three
     back_two = gather_rows(back_hidden_two.astype(jnp.bfloat16))
     back_attended = (
         product_right(back_two, mix_w[5]).astype(jnp.bfloat16).reshape(length, local_heads, HEAD)

time: 908 us -> 861 us (0.948)
  the two profiles are of different devices: /device:TPU:12 before, /device:TPU:0 now
where the time goes in v2:
time: 861 us; the launch traced here: 849 us
  Pallas kernels  572 us (66%)
  waiting for transfers between devices  122 us (14%)
  matrix products  58.5 us (7%)
  local copies, waits for them, and re-layouts  34.9 us (4%)
  other arithmetic  30.7 us (4%)
  starting transfers between devices  15.6 us (2%)
  between operations  15 us (2%)
    pallas_call x1, Pallas kernels, scatter_sum(): pl.pallas_call(functools.partial(scatter_body, owners, caps, tuple(jobs))...  256 us
    pallas_call x1, Pallas kernels, spread_units(): pl.pallas_call(functools.partial(spread_body, owners, cap, jobs), out_sha...  151 us
    ppermute x12, waiting for transfers between devices, swap(): return lax.ppermute(values, axis, [(i, i ^ bit) for i in range(size)])  76.7 us
    pallas_call x3, Pallas kernels, grad_units(): pl.pallas_call(functools.partial(grad_body, tuple(parts), len(operands)),...  60.8 us
    all_gather x1, waiting for transfers between devices, per_device(): lax.all_gather(own_mlp, 'dp', axis=0, tiled=True)  39.8 us
    pallas_call x1, Pallas kernels, feed_forward(): pl.pallas_call(functools.partial(ffn_body, wide), grid_spec=pltpu.Prefetc...  36.5 us
    pallas_call x2, Pallas kernels, lay_out(): pl.pallas_call(functools.partial(lay_body, tuple(parts)), grid_spec=pltpu...  35.7 us
    pallas_call x3, Pallas kernels, adam_units(): pl.pallas_call(functools.partial(adam_body, scale), grid=(unit_width // b...  31.5 us
  transfers between devices with their start and end apart: 15, of which 11 were waited for; matrix products, arithmetic and copies ran while one was open for 12% of the time, Pallas kernels for 58%

profile of v2, /device:TPU:0, one launch (start us, length us, event | category | flops | bytes accessed | tf_op | source)
XLA Modules:
  0.0 848.8 jit_solution(14390561210667946500)
XLA Ops:
  7.2 2.4 multiply_convert_fusion
  11.7 1.9 multiply_convert_fusion.1
  19.7 3.1 collective-permute-start
  22.8 151.1 %spread_23.1 = bf16[16,23,128,128]{3,2,1,0:T(8,128)(2,1)} custom-call(bf16[23,128,128]{2,1,0:T(8,128)(2,1)} %slice.118.own_ref), custom_call_target="tpu_custom_call" | custom-call | tf_op jit(solution)/shard_map/spread_23/pallas_call | solution.py:718
  174.0 16.3 %lay_294.1 = (bf16[3584,896]{1,0:T(8,128)(2,1)}, bf16[896,1792]{1,0:T(8,128)(2,1)}) custom-call(s32[294]{0:T(512)} %slots_ref.10, bf16[368,128,128]{2,1,0:T(8,128)(2,1)} %bitcast.150), custom_call_target="tpu_custom_call" | custom-call | bytes 19267584 | tf_op jit(solution)/shard_map/lay_294/pallas_call | solution.py:166
  190.8 3.6 fusion.20
  195.3 2.4 multiply_convert_fusion.8
  199.6 12.0 %collective-permute-done.1 = bf16[128,1792]{1,0:T(8,128)(2,1)S(1)} collective-permute-done((bf16[128,1792]{1,0:T(8,128)(2,1)S(1)}, bf16[128,1792]{1,0:T(8,128)(2,1)S(1)}, u32[]{:S(2)}, u32[]{:S(2)}) %collective-permute-start.1) | collective-permute-done | bytes 458784 | tf_op jit(solution)/shard_map/ppermute | solution.py:66
  213.8 10.2 %collective-permute-done.2 = bf16[128,1792]{1,0:T(8,128)(2,1)S(1)} collective-permute-done((bf16[128,1792]{1,0:T(8,128)(2,1)S(1)}, bf16[128,1792]{1,0:T(8,128)(2,1)S(1)}, u32[]{:S(2)}, u32[]{:S(2)}) %collective-permute-start.2) | collective-permute-done | bytes 458784 | tf_op jit(solution)/shard_map/ppermute | solution.py:66
  224.3 19.5 %lay_420.1 = (bf16[3584,128]{1,0:T(8,128)(2,1)}, bf16[5376,896]{1,0:T(8,128)(2,1)}, bf16[896,1792]{1,0:T(8,128)(2,1)}) custom-call(s32[420]{0:T(512)} %slots_ref.9, bf16[528,128,128]{2,1,0:T(8,128)(2,1)} %all-gather.3.cloned.1.call-done.pooled_ref), custom_call_target="tpu_custom_call" | custom-call | bytes 27525120 | tf_op jit(solution)/shard_map/lay_420/pallas_call | solution.py:166
  243.8 3.1 fusion.49
  247.8 3.1 fusion.55
  251.9 4.1 fusion.52
  256.0 2.0 copy.82
  259.0 2.0 fusion.48
  261.0 2.6 fusion.133
  263.6 3.3 fusion.95
  267.3 1.7 copy-done.50
  272.3 11.4 %collective-permute-done.3 = bf16[128,1792]{1,0:T(8,128)(2,1)S(1)} collective-permute-done((bf16[128,1792]{1,0:T(8,128)(2,1)S(1)}, bf16[128,1792]{1,0:T(8,128)(2,1)S(1)}, u32[]{:S(2)}, u32[]{:S(2)}) %collective-permute-start.3) | collective-permute-done | bytes 458784 | tf_op jit(solution)/shard_map/ppermute | solution.py:66
  285.4 8.1 collective-permute-done.5
  293.6 7.4 collective-permute-done.4
  302.6 39.8 %all-gather.5.cloned.1.call-done.pooled_ref = bf16[1008,128,128]{2,1,0:T(8,128)(2,1)} async-done(((bf16[63,128,128]{2,1,0:T(8,128)(2,1)}), bf16[1008,128,128]{2,1,0:T(8,128)(2,1)}) %all-gather.5.cloned.1.call-update) | async-done | bytes 33030160 | tf_op jit(solution)/shard_map/all_gather | solution.py:788
  342.5 36.5 %feed_forward.1 = (bf16[256,1792]{1,0:T(8,128)(2,1)}, bf16[256,2432]{1,0:T(8,128)(2,1)}, bf16[256,2432]{1,0:T(8,128)(2,1)}, bf16[256,2432]{1,0:T(8,128)(2,1)}, bf16[256,1792]{1,0:T(8,128)(2,1)}) custom-call(s32[798]{0:T(1024)} %slots_ref.11, bf16[1008,128,128]{2,1,0:T(8,128)(2,1)} %all-gather.5.cloned.1.call-done.pooled_ref, ...), custom_call_target="tpu_custom_call" | custom-call | flops 13388218368 | bytes 26148864 | tf_op jit(solution)/shard_map/feed_forward/pallas_call | solution.py:290
  379.0 26.1 %grad_798.1 = bf16[1008,128,128]{2,1,0:T(8,128)(2,1)} custom-call(s32[798]{0:T(1024)} %slots_ref.11, bf16[256,1792]{1,0:T(8,128)(2,1)} %get-tuple-element.121.u_ref.refs_0_, bf16[256,2432]{1,0:T(8,128)(2,1)} %get-tuple-element.35.refs_1_, bf16[256,2432]{1,0:T(8,128)(2,1)} %get-tuple-element.36.refs_2_, bf16[256,2432]{1,0:T(8,128)(2,1)} %get-tuple-element.37.refs_3_, ...), custom_call_target="tpu_custom_call" | custom-call | flops 6694109184 | bytes 26148864 | tf_op jit(solution)/shard_map/grad_798/pallas_call | solution.py:386
  405.2 1.8 dynamic-slice_bitcast_fusion.2
  408.9 10.9 %collective-permute-done.7 = bf16[128,1792]{1,0:T(8,128)(2,1)S(1)} collective-permute-done((bf16[128,1792]{1,0:T(8,128)(2,1)}, bf16[128,1792]{1,0:T(8,128)(2,1)S(1)}, u32[]{:S(2)}, u32[]{:S(2)}) %collective-permute-start.7) | collective-permute-done | bytes 458784 | tf_op jit(solution)/shard_map/ppermute | solution.py:66
  424.7 9.0 %collective-permute-done.8 = bf16[128,1792]{1,0:T(8,128)(2,1)S(1)} collective-permute-done((bf16[128,1792]{1,0:T(8,128)(2,1)S(1)}, bf16[128,1792]{1,0:T(8,128)(2,1)S(1)}, u32[]{:S(2)}, u32[]{:S(2)}) %collective-permute-start.8) | collective-permute-done | bytes 458784 | tf_op jit(solution)/shard_map/ppermute | solution.py:66
  434.8 1.9 convolution_convert_fusion.2
  438.0 3.9 multiply_reduce_fusion
  442.0 6.4 fusion.63
  448.3 6.3 fusion.62
  454.6 2.7 multiply_convert_fusion.2
  463.8 2.0 slice-done.1
  471.6 1.7 collective-permute-start.9
  475.5 2.0 copy.97.refs_6_
  477.5 2.0 copy.96.refs_5_
  483.1 2.2 collective-permute-done.9
  486.8 5.4 collective-permute-done.6
  492.2 3.4 fusion.130
  495.7 1.6 collective-permute-start.10
  498.3 20.2 %grad_420.1 = bf16[528,128,128]{2,1,0:T(8,128)(2,1)} custom-call(s32[420]{0:T(512)} %slots_ref.9, bf16[256,1792]{1,0:T(8,128)(2,1)} %pad_maximum_fusion.1.refs_0_, bf16[256,128]{1,0:T(8,128)(2,1)} %copy.92.refs_1_, bf16[256,128]{1,0:T(8,128)(2,1)} %copy.93.refs_2_, bf16[256,896]{1,0:T(8,128)(2,1)} %copy.94.refs_3_, bf16[256,896]{1,0:T(8,128)(2,1)} %copy.95.refs_4_, ...), custom_call_target="tpu_custom_call" | custom-call | flops 3523215360 | bytes 13762560 | tf_op jit(solution)/shard_map/grad_420/pallas_call | solution.py:386
  520.1 3.6 multiply_reduce_fusion.4
  528.3 14.5 %grad_294.1 = bf16[368,128,128]{2,1,0:T(8,128)(2,1)} custom-call(s32[294]{0:T(512)} %slots_ref.10, bf16[256,1792]{1,0:T(8,128)(2,1)} %pad_maximum_fusion.refs_0_, bf16[256,896]{1,0:T(8,128)(2,1)} %copy-done.26, bf16[256,896]{1,0:T(8,128)(2,1)} %copy-done.27, bf16[256,896]{1,0:T(8,128)(2,1)} %copy-done.41, bf16[256,1792]{1,0:T(8,128)(2,1)} %pad_maximum_fusion.5.refs_4_), custom_call_target="tpu_custom_call" | custom-call | flops 2466250752 | bytes 9633792 | tf_op jit(solution)/shard_map/grad_294/pallas_call | solution.py:386
  544.0 256.0 %scatter_sum.1 = (f32[33,128,128]{2,1,0:T(8,128)}, f32[23,128,128]{2,1,0:T(8,128)}, f32[6,1792]{1,0:T(8,128)}) custom-call(bf16[8,2,33,128,128]{4,3,2,1,0:T(8,128)(2,1)} %bitcast.148, bf16[8,2,23,128,128]{4,3,2,1,0:T(8,128)(2,1)} %bitcast.149, f32[6,1792]{1,0:T(8,128)} %pad_maximum_fusion.7.refs_2_), custom_call_target="tpu_custom_call" | custom-call | tf_op jit(solution)/shard_map/scatter_sum/pallas_call | solution.py:576
  802.9 9.9 %adam_33.1 = f32[3,33,16384]{2,1,0:T(8,128)} custom-call(s32[33,128]{1,0:T(8,128)} %broadcast_in_dim.35.used_ref, f32[3,33,16384]{2,1,0:T(8,128)} %state_ref.4, f32[33,128,128]{2,1,0:T(8,128)} %get-tuple-element.34.summed_ref), custom_call_target="tpu_custom_call" | custom-call | tf_op jit(solution)/shard_map/adam_33/pallas_call | solution.py:635
  813.5 7.8 adam_23.1
  822.6 5.1 reduce-scatter.4.cloned.1.call-done.summed_ref
  828.3 13.8 %adam_63.1 = f32[3,63,16384]{2,1,0:T(8,128)} custom-call(s32[63,128]{1,0:T(8,128)} %broadcast_in_dim.36.used_ref, f32[3,63,16384]{2,1,0:T(8,128)} %state_ref.5, bf16[63,128,128]{2,1,0:T(8,128)(2,1)} %reduce-scatter.4.cloned.1.call-done.summed_ref), custom_call_target="tpu_custom_call" | custom-call | tf_op jit(solution)/shard_map/adam_63/pallas_call | solution.py:635
  (237 shorter events, 65.9 us)
Async XLA Ops:
  7.2 217.1 %all-gather.3.cloned.1.call-start = ((), (), s32[]{:S(2)}) async-start(), calls=%async_computation.1 | async-start | bytes 18382848 | tf_op jit(solution)/shard_map/all_gather | solution.py:787
  17.7 324.8 %all-gather.5.cloned.1.call-start = ((), (), s32[]{:S(2)}) async-start(), calls=%async_computation.2 | async-start | bytes 35094528 | tf_op jit(solution)/shard_map/all_gather | solution.py:788
  18.4 809.2 %reduce-scatter.4.cloned.1.call-start = ((), (), s32[]{:S(2)}) async-start(), calls=%async_computation.3 | async-start | bytes 35094528
  19.7 170.7 %collective-permute-start = (bf16[128,1792]{1,0:T(8,128)(2,1)S(1)}, bf16[128,1792]{1,0:T(8,128)(2,1)S(1)}, u32[]{:S(2)}, u32[]{:S(2)}) collective-permute-start(bf16[128,1792]{1,0:T(8,128)(2,1)S(1)} %fusion.78), channel_id=1, source_target_pairs={{0,1},{1,0},{2,3},{3,2},{4,5},{5,4},{6,7},{7,6},{8,9},{9,8},{10,11... | collective-permute-start | bytes 1376264 | tf_op jit(solution)/shard_map/ppermute | solution.py:66
  174.0 16.4 %copy-start.48 = (s32[1,256]{1,0:T(1,128)S(1)}, s32[1,256]{1,0:T(1,128)}, u32[]{:S(2)}) copy-start(s32[1,256]{1,0:T(1,128)} %param.12) | copy-start | bytes 3076
  190.8 3.7 copy-start.12
  190.8 3.7 copy-start.14
  190.8 4.5 copy-start.49
  198.9 12.7 %collective-permute-start.1 = (bf16[128,1792]{1,0:T(8,128)(2,1)S(1)}, bf16[128,1792]{1,0:T(8,128)(2,1)S(1)}, u32[]{:S(2)}, u32[]{:S(2)}) collective-permute-start(bf16[128,1792]{1,0:T(8,128)(2,1)S(1)} %dynamic-slice_bitcast_fusion.5), channel_id=1, source_target_pairs={{0,1},{1,0},{2,3},{3,2},{4,5},{5,4},{6,7},{7,6},{8,9},{9,8},{10,11... | collective-permute-start | bytes 1376264 | tf_op jit(solution)/shard_map/ppermute | solution.py:66
  212.1 11.9 %collective-permute-start.2 = (bf16[128,1792]{1,0:T(8,128)(2,1)S(1)}, bf16[128,1792]{1,0:T(8,128)(2,1)S(1)}, u32[]{:S(2)}, u32[]{:S(2)}) collective-permute-start(bf16[128,1792]{1,0:T(8,128)(2,1)S(1)} %multiply_convert_fusion.7), channel_id=1, source_target_pairs={{0,1},{1,0},{2,3},{3,2},{4,5},{5,4},{6,7},{7,6},{8,9},{9,8},{10,11... | collective-permute-start | bytes 1376264 | tf_op jit(solution)/shard_map/ppermute | solution.py:66
  213.8 45.2 %copy-start.43 = (f32[256,256]{0,1:T(8,128)}, f32[256,256]{0,1:T(8,128)S(1)}, u32[]{:S(2)}) copy-start(f32[256,256]{0,1:T(8,128)S(1)} %get-tuple-element.111) | copy-start | bytes 786436
  224.3 34.2 %copy-start.16 = (bf16[128,1792]{1,0:T(8,128)(2,1)}, bf16[128,1792]{1,0:T(8,128)(2,1)S(1)}, u32[]{:S(2)}) copy-start(bf16[128,1792]{1,0:T(8,128)(2,1)S(1)} %get-tuple-element.103) | copy-start | bytes 1376260
  224.3 34.2 %copy-start.18 = (bf16[128,1792]{1,0:T(8,128)(2,1)}, bf16[128,1792]{1,0:T(8,128)(2,1)S(1)}, u32[]{:S(2)}) copy-start(bf16[128,1792]{1,0:T(8,128)(2,1)S(1)} %get-tuple-element.104) | copy-start | bytes 1376260
  251.9 6.1 copy-start.33
  270.2 13.5 %collective-permute-start.3 = (bf16[128,1792]{1,0:T(8,128)(2,1)S(1)}, bf16[128,1792]{1,0:T(8,128)(2,1)S(1)}, u32[]{:S(2)}, u32[]{:S(2)}) collective-permute-start(bf16[128,1792]{1,0:T(8,128)(2,1)S(1)} %dynamic-slice_bitcast_fusion.4), channel_id=1, source_target_pairs={{0,1},{1,0},{2,3},{3,2},{4,5},{5,4},{6,7},{7,6},{8,9},{9,8},{10,11... | collective-permute-start | bytes 1376264 | tf_op jit(solution)/shard_map/ppermute | solution.py:66
  271.5 22.0 %collective-permute-start.5 = (bf16[128,1792]{1,0:T(8,128)(2,1)S(1)}, bf16[128,1792]{1,0:T(8,128)(2,1)S(1)}, u32[]{:S(2)}, u32[]{:S(2)}) collective-permute-start(bf16[128,1792]{1,0:T(8,128)(2,1)S(1)} %copy-done.1), channel_id=1, source_target_pairs={{0,1},{1,0},{2,3},{3,2},{4,5},{5,4},{6,7},{7,6},{8,9},{9,8},{10,11... | collective-permute-start | bytes 1376264 | tf_op jit(solution)/shard_map/ppermute | solution.py:66
  284.2 16.8 %collective-permute-start.4 = (bf16[128,1792]{1,0:T(8,128)(2,1)S(1)}, bf16[128,1792]{1,0:T(8,128)(2,1)S(1)}, u32[]{:S(2)}, u32[]{:S(2)}) collective-permute-start(bf16[128,1792]{1,0:T(8,128)(2,1)S(1)} %multiply_convert_fusion.6), channel_id=1, source_target_pairs={{0,1},{1,0},{2,3},{3,2},{4,5},{5,4},{6,7},{7,6},{8,9},{9,8},{10,11... | collective-permute-start | bytes 1376264 | tf_op jit(solution)/shard_map/ppermute | solution.py:66
  405.1 3.6 copy-start.46
  407.0 12.9 %collective-permute-start.7 = (bf16[128,1792]{1,0:T(8,128)(2,1)}, bf16[128,1792]{1,0:T(8,128)(2,1)S(1)}, u32[]{:S(2)}, u32[]{:S(2)}) collective-permute-start(bf16[128,1792]{1,0:T(8,128)(2,1)} %dynamic-slice_bitcast_fusion.2), channel_id=1, source_target_pairs={{0,1},{1,0},{2,3},{3,2},{4,5},{5,4},{6,7},{7,6},{8,9},{9,8},{10,11... | collective-permute-start | bytes 1376264 | tf_op jit(solution)/shard_map/ppermute | solution.py:66
  408.9 12.6 %copy-start.5 = (bf16[256,1792]{1,0:T(8,128)(2,1)S(1)}, bf16[256,1792]{1,0:T(8,128)(2,1)}, u32[]{:S(2)}) copy-start(bf16[256,1792]{1,0:T(8,128)(2,1)} %get-tuple-element.32) | copy-start | bytes 2752516
  408.9 14.5 %copy-start.45 = (s32[294]{0:T(512)S(1)}, s32[294]{0:T(512)}, u32[]{:S(2)}) copy-start(s32[294]{0:T(512)} %slots_ref.10) | copy-start | bytes 3532
  408.9 14.7 %copy-start.13 = (bf16[128,1792]{1,0:T(8,128)(2,1)S(1)}, bf16[128,1792]{1,0:T(8,128)(2,1)}, u32[]{:S(2)}) copy-start(bf16[128,1792]{1,0:T(8,128)(2,1)} %copy-done.12) | copy-start | bytes 1376260
  408.9 14.7 %copy-start.15 = (bf16[128,1792]{1,0:T(8,128)(2,1)S(1)}, bf16[128,1792]{1,0:T(8,128)(2,1)}, u32[]{:S(2)}) copy-start(bf16[128,1792]{1,0:T(8,128)(2,1)} %copy-done.14) | copy-start | bytes 1376260
  421.8 13.0 %copy-start.51 = (bf16[896,1792]{1,0:T(8,128)(2,1)S(1)}, bf16[896,1792]{1,0:T(8,128)(2,1)}, u32[]{:S(2)}) copy-start(bf16[896,1792]{1,0:T(8,128)(2,1)} %get-tuple-element.29) | copy-start | bytes 9633796
  421.8 11.9 %collective-permute-start.8 = (bf16[128,1792]{1,0:T(8,128)(2,1)S(1)}, bf16[128,1792]{1,0:T(8,128)(2,1)S(1)}, u32[]{:S(2)}, u32[]{:S(2)}) collective-permute-start(bf16[128,1792]{1,0:T(8,128)(2,1)S(1)} %fusion.123), channel_id=1, source_target_pairs={{0,1},{1,0},{2,3},{3,2},{4,5},{5,4},{6,7},{7,6},{8,9},{9,8},{10,11... | collective-permute-start | bytes 1376264 | tf_op jit(solution)/shard_map/ppermute | solution.py:66
  438.0 4.0 copy-start.39
  438.0 4.0 copy-start.55
  442.0 6.4 copy-start.53
  461.0 4.8 slice-start.1
  462.5 3.7 slice-start.2
  463.0 5.7 copy-start.38
  468.7 4.6 copy-start.32
  469.9 4.6 copy-start.17
  469.9 4.6 copy-start.19
  471.6 13.7 %collective-permute-start.9 = (bf16[128,1792]{1,0:T(8,128)(2,1)}, bf16[128,1792]{1,0:T(8,128)(2,1)}, u32[]{:S(2)}, u32[]{:S(2)}) collective-permute-start(bf16[128,1792]{1,0:T(8,128)(2,1)} %dynamic-slice_bitcast_fusion.1), channel_id=1, source_target_pairs={{0,1},{1,0},{2,3},{3,2},{4,5},{5,4},{6,7},{7,6},{8,9},{9,8},{10,11... | collective-permute-start | bytes 1376264 | tf_op jit(solution)/shard_map/ppermute | solution.py:66
  474.1 18.1 %collective-permute-start.6 = (bf16[128,1792]{1,0:T(8,128)(2,1)}, bf16[128,1792]{1,0:T(8,128)(2,1)}, u32[]{:S(2)}, u32[]{:S(2)}) collective-permute-start(bf16[128,1792]{1,0:T(8,128)(2,1)} %dynamic-slice_bitcast_fusion.3), channel_id=1, source_target_pairs={{0,1},{1,0},{2,3},{3,2},{4,5},{5,4},{6,7},{7,6},{8,9},{9,8},{10,11... | collective-permute-start | bytes 1376264 | tf_op jit(solution)/shard_map/ppermute | solution.py:66
  480.5 11.8 %copy-start.2 = (bf16[128,1792]{1,0:T(8,128)(2,1)S(1)}, bf16[128,1792]{1,0:T(8,128)(2,1)}, u32[]{:S(2)}) copy-start(bf16[128,1792]{1,0:T(8,128)(2,1)} %param.11) | copy-start | bytes 1376260
  481.5 10.8 %copy-start.4 = (bf16[128,1792]{1,0:T(8,128)(2,1)S(1)}, bf16[128,1792]{1,0:T(8,128)(2,1)}, u32[]{:S(2)}) copy-start(bf16[128,1792]{1,0:T(8,128)(2,1)} %copy-done.3) | copy-start | bytes 1376260
  483.1 9.1 %copy-start.6 = (bf16[256,1792]{1,0:T(8,128)(2,1)S(1)}, bf16[256,1792]{1,0:T(8,128)(2,1)}, u32[]{:S(2)}) copy-start(bf16[256,1792]{1,0:T(8,128)(2,1)} %get-tuple-element.32) | copy-start | bytes 2752516
  486.8 10.5 %copy-start.23 = (bf16[128,1792]{1,0:T(8,128)(2,1)S(1)}, bf16[128,1792]{1,0:T(8,128)(2,1)}, u32[]{:S(2)}) copy-start(bf16[128,1792]{1,0:T(8,128)(2,1)} %copy-done.22) | copy-start | bytes 1376260
  486.8 10.5 %copy-start.25 = (bf16[128,1792]{1,0:T(8,128)(2,1)S(1)}, bf16[128,1792]{1,0:T(8,128)(2,1)}, u32[]{:S(2)}) copy-start(bf16[128,1792]{1,0:T(8,128)(2,1)} %copy-done.24) | copy-start | bytes 1376260
  495.7 22.9 %collective-permute-start.10 = (bf16[128,1792]{1,0:T(8,128)(2,1)}, bf16[128,1792]{1,0:T(8,128)(2,1)S(1)}, u32[]{:S(2)}, u32[]{:S(2)}) collective-permute-start(bf16[128,1792]{1,0:T(8,128)(2,1)} %get-tuple-element.85), channel_id=1, source_target_pairs={{0,1},{1,0},{2,3},{3,2},{4,5},{5,4},{6,7},{7,6},{8,9},{9,8},{10,11... | collective-permute-start | bytes 1376264 | tf_op jit(solution)/shard_map/ppermute | solution.py:66
  498.3 21.5 %copy-start.31 = (f32[256,896]{1,0:T(8,128)S(1)}, f32[256,896]{1,0:T(8,128)}, u32[]{:S(2)}) copy-start(f32[256,896]{1,0:T(8,128)} %get-tuple-element.114) | copy-start | bytes 2752516
  519.8 4.3 slice-start.3
  520.1 4.0 slice-start.4
  526.6 16.2 %collective-permute-start.11 = (bf16[128,1792]{1,0:T(8,128)(2,1)S(1)}, bf16[128,1792]{1,0:T(8,128)(2,1)S(1)}, u32[]{:S(2)}, u32[]{:S(2)}) collective-permute-start(bf16[128,1792]{1,0:T(8,128)(2,1)S(1)} %dynamic-slice_bitcast_fusion), channel_id=1, source_target_pairs={{0,1},{1,0},{2,3},{3,2},{4,5},{5,4},{6,7},{7,6},{8,9},{9,8},{10,11... | collective-permute-start | bytes 1376264 | tf_op jit(solution)/shard_map/ppermute | solution.py:66
  544.0 256.0 %copy-start.42 = (f32[3,6,1792]{2,1,0:T(8,128)S(1)}, f32[3,6,1792]{2,1,0:T(8,128)}, u32[]{:S(2)}) copy-start(f32[3,6,1792]{2,1,0:T(8,128)} %param.19) | copy-start | bytes 387076
  813.5 7.9 copy-start.7
  (29 other events, 58.4 us)
Sparse Core Ops, SparseCore 0:
  17.8 154.7 all-gather.2
  174.1 168.2 all-gather.4
  405.3 422.3 reduce-scatter.3
